TPU v7x, 32 devices: a whole 2x2x4 slice. The times are simulated.
32 devices in a mesh: span: 2 (over y), height: 4 (over x, core), depth: 4 (over z).
Axes of the slice: x: 2, y: 2, z: 4, core: 2. Of those that a mesh axis runs over, the one named last changes fastest.
Arguments:
- load: float32 [8, 32, 64, 512], P(None, 'span', 'height', 'depth'), may hold values from -6 to 6
- phase: float32 [32, 64, 512], P('span', 'height', 'depth'), may hold values from 0.1 to 1
- void: int32 [4, 8, 64], P('span', 'height', 'depth'), may hold values from 0 to 1, as said below
- owner: int32 [4, 8, 64], P('span', 'height', 'depth'), may hold values from 0 to 1, as said below
- precond: bfloat16 [512, 512, 512], P(('span', 'height', 'depth')), may hold values from -1 to 2, as said below
Outputs:
- displacement: float32 [8, 32, 64, 512], P(None, 'span', 'height', 'depth')
- sensitivity: float32 [32, 64, 512], P('span', 'height', 'depth')
- phase_next: float32 [32, 64, 512], P('span', 'height', 'depth')
Inputs may be any that keep to these rules, and one draw needn't show every extreme that they name: `void`: each device's block of 16 x 16 x 128 cells holds at most 16 solid bricks; some device holds exactly 16. `owner`: among the solid bricks of one device at most 8 name any one value; on some device every value is named by exactly 8 solid bricks. Values of void bricks carry no meaning. `precond`: every block is symmetric with a positive diagonal that dominates each row.
All inputs are finite; a program needn't handle non-finite values.
Results may differ from a plain program's by a relative error of at most 0.0021.
Values may be sent and summed in bfloat16 or wider, within the bound.
No kernel may reach another device: no remote copies, remote signals or barrier semaphores. Data moves between devices by JAX's collectives and lax.ppermute only.
A program may use at most 128 MiB of HBM per device.

v0:
```python
import jax
import jax.numpy as jnp
from jax import lax
from jax.sharding import PartitionSpec as P

BE = 8
ITERS = 2
SWEEPS = 2
void_stiffness = 0.001
spring_rate = 0.05
time_step = 0.5
interface_weight = 0.5
epsilon_peak = 1e-06


def padded_2(block, sides, width):
    for axis, dim in sides:
        count = lax.axis_size(axis)
        forward = [(i, i + 1) for i in range(count - 1)]
        backward = [(target, source) for source, target in forward]
        low = lax.ppermute(
            lax.slice_in_dim(block, block.shape[dim] - width, None, axis=dim), axis, forward
        )
        high = lax.ppermute(lax.slice_in_dim(block, 0, width, axis=dim), axis, backward)
        block = jnp.concatenate([low, block, high], axis=dim)
    return block


def neighbours(padded):
    return [
        padded[..., 2:, 1:-1, 1:-1],
        padded[..., :-2, 1:-1, 1:-1],
        padded[..., 1:-1, 2:, 1:-1],
        padded[..., 1:-1, :-2, 1:-1],
        padded[..., 1:-1, 1:-1, 2:],
        padded[..., 1:-1, 1:-1, :-2],
    ]


def halo_stack(stacked):
    return padded_2(stacked, (("span", 1), ("height", 2), ("depth", 3)), 1)


def cell_sums(first, second):
    return jnp.sum(first * second, axis=(1, 2, 3))


def paired_sums(residual, search, image):
    return lax.psum(
        (cell_sums(residual, search), cell_sums(image, search)), ("span", "height", "depth")
    )


def local(load, phase, void, owner, precond):
    extents = phase.shape
    bricks_x, bricks_y, bricks_z = void.shape
    solid_bricks = (1 - void).astype(jnp.float32)
    expanded = jnp.broadcast_to(
        solid_bricks[:, None, :, None, :, None], (bricks_x, BE, bricks_y, BE, bricks_z, BE)
    )
    cell_mask = expanded.reshape(extents)
    stiffness = void_stiffness + (1.0 - void_stiffness) * phase**3
    coefficients = halo_stack(jnp.stack([cell_mask, cell_mask * stiffness]))
    near_pairs = neighbours(coefficients)
    weights = [cell_mask * 0.5 * (pair[0] * stiffness + pair[1]) for pair in near_pairs]

    def operate(field):
        padded = halo_stack(field)
        total = cell_mask * spring_rate * field
        for weight, near in zip(weights, neighbours(padded)):
            total = total + weight * (field - near)
        return (total, padded)

    span_count = lax.axis_size("span")
    slot_count = precond.shape[0]
    capacity = slot_count // span_count
    solid_flat = (1 - void).reshape(-1)
    owner_flat = owner.reshape(-1)
    columns = jnp.arange(span_count, dtype=jnp.int32)
    onehot = (owner_flat[:, None] == columns[None, :]).astype(jnp.int32) * solid_flat[:, None]
    before = jnp.cumsum(onehot, axis=0) - onehot
    rank = jnp.sum(before * onehot, axis=1)
    slot_of_brick = owner_flat * capacity + rank
    slot_ids = jnp.arange(slot_count, dtype=jnp.int32)
    matched = (slot_of_brick[None, :] == slot_ids[:, None]).astype(jnp.float32) * solid_flat[
        None, :
    ].astype(jnp.float32)
    selector = matched.reshape(slot_count, bricks_x, bricks_y, bricks_z)
    selector_low = selector.astype(jnp.bfloat16)
    loads = load.shape[0]

    def apply_blocks(incoming):
        image = jnp.einsum("sij,slj->sli", precond, incoming, preferred_element_type=jnp.float32)
        return lax.all_to_all(image, "span", split_axis=0, concat_axis=0, tiled=True)

    def precondition(residual):
        split = residual.astype(jnp.bfloat16).reshape(
            loads, bricks_x, BE, bricks_y, BE, bricks_z, BE
        )
        outgoing = jnp.einsum(
            "sxyz,lxiyjzk->slijk", selector_low, split, preferred_element_type=jnp.float32
        )
        outgoing = outgoing.astype(jnp.bfloat16).reshape(slot_count, loads, BE**3)
        returned = apply_blocks(
            lax.all_to_all(outgoing, "span", split_axis=0, concat_axis=0, tiled=True)
        )
        shaped = returned.reshape(slot_count, loads, BE, BE, BE)
        placed = jnp.einsum(
            "sxyz,slijk->lxiyjzk", selector, shaped, precision=lax.Precision.HIGHEST
        )
        return placed.reshape(loads, extents[0], extents[1], extents[2])

    right_side = cell_mask[None] * load
    solution = jnp.zeros_like(right_side)
    padded_solution = 0.0
    residual = right_side
    search = precondition(residual)
    image, padded_search = operate(search)
    norm_now, curvature_sum = paired_sums(residual, search, image)
    step_size = norm_now / curvature_sum
    direction = search
    padded_direction = padded_search
    along = image
    for iteration in range(ITERS):
        solution = solution + step_size[:, None, None, None] * direction
        padded_solution = padded_solution + step_size[:, None, None, None] * padded_direction
        residual = residual - step_size[:, None, None, None] * along
        if iteration + 1 < ITERS:
            search = precondition(residual)
            image, padded_search = operate(search)
            norm_next, curvature_sum = paired_sums(residual, search, image)
            factor = norm_next / norm_now
            step_size = norm_next / (curvature_sum - factor * norm_next / step_size)
            direction = search + factor[:, None, None, None] * direction
            padded_direction = padded_search + factor[:, None, None, None] * padded_direction
            along = image + factor[:, None, None, None] * along
            norm_now = norm_next
    solution_padded = halo_stack(solution)
    energy = jnp.zeros_like(phase)
    for pair, near in zip(near_pairs, neighbours(solution_padded)):
        energy = energy + pair[0] * jnp.sum((solution - near) ** 2, axis=0)
    sensitivity = -1.5 * (1.0 - void_stiffness) * phase**2 * cell_mask * energy
    peak_value = lax.pmax(jnp.max(-sensitivity), ("span", "height", "depth"))
    drive = (
        phase / time_step
        - 0.5 * phase * (1.0 - phase) * (1.0 - 2.0 * phase)
        - sensitivity / (peak_value + epsilon_peak)
    )
    inverse = 1.0 / (1.0 / time_step + 6.0 * interface_weight)
    current = phase
    for sweep_index in range(SWEEPS):
        padded = padded_2(
            current.astype(jnp.bfloat16), (("span", 0), ("height", 1), ("depth", 2)), 1
        ).astype(current.dtype)
        beside_all = neighbours(padded)
        current = (
            drive
            + interface_weight
            * (
                beside_all[0]
                + beside_all[1]
                + beside_all[2]
                + beside_all[3]
                + beside_all[4]
                + beside_all[5]
            )
        ) * inverse
    return (solution, sensitivity, current)


def solution(mesh):
    return jax.shard_map(
        local,
        mesh=mesh,
        in_specs=(
            P(None, "span", "height", "depth"),
            P("span", "height", "depth"),
            P("span", "height", "depth"),
            P("span", "height", "depth"),
            P(("span", "height", "depth"), None, None),
        ),
        out_specs=(
            P(None, "span", "height", "depth"),
            P("span", "height", "depth"),
            P("span", "height", "depth"),
        ),
        check_vma=False,
    )
```

profile of v0, /device:TPU:14, one launch (start us, length us, event | category | flops | bytes accessed | tf_op | source)
XLA Modules:
  0.0 461.7 jit_solution(4808410751461738423)
XLA Ops:
  5.8 2.4 collective-permute-start
  10.2 10.6 %reshape.116 = bf16[8,2,8,2,8,16,8]{6,5,4,3,2,1,0:T(8,128)(2,1)} reshape(bf16[8,16,16,128]{3,2,1,0:T(8,128)(2,1)S(1)} %multiply_convert_fusion) | data formatting | bytes 1048576 | tf_op jit(solution)/shard_map/reshape | solution.py:97
  22.8 2.4 collective-permute-start.6
  25.2 6.2 %bitcast_convert_fusion.1 = bf16[16,8,8,8,8]{0,4,3,2,1:T(8,128)(2,1)S(1)} fusion(bf16[8,2,8,2,8,16,8]{6,5,4,3,2,1,0:T(8,128)(2,1)} %reshape.116, f32[2,2,16]{2,1,0:T(2,128)S(1)} %copy-done.42, s32[2,2,16]{2,1,0:T(2,128)S(1)} %multiply_add_fusion.1), kind=kOutput, calls=%fused_computation.3 | convolution fusion | flops 8456192 | bytes 655872 | tf_op jit(solution)/shard_map/sxyz,lxiyjzk->slijk/dot_general | solution.py:100
  32.5 6.0 %all-to-all-start = ((bf16[16,8,512]{2,1,0:T(8,128)(2,1)}), bf16[16,8,512]{2,1,0:T(8,128)(2,1)S(1)}, u32[]{:S(2)}, u32[]{:S(2)}) async-start(bf16[16,8,512]{2,1,0:T(8,128)(2,1)} %copy.23), calls=%async_computation | async-start | bytes 262144 | tf_op jit(solution)/shard_map/all_to_all | solution.py:105
  39.6 3.5 collective-permute-start.10
  43.1 3.2 collective-permute-start.8
  46.3 6.4 %fusion.123 = f32[16,8,512]{2,1,0:T(8,128)} fusion(bf16[16,8,512]{2,1,0:T(8,128)(2,1)S(1)} %all-to-all-done, bf16[16,512,512]{2,1,0:T(8,128)(2,1)} %param.9), kind=kOutput, calls=%fused_computation.250 | convolution fusion | flops 67108864 | bytes 8781824 | tf_op jit(solution)/shard_map/sij,slj->sli/dot_general | solution.py:93
  52.7 4.6 all-to-all-start.1
  58.2 2.4 all-to-all-done.1
  62.1 9.5 %convolution_bitcast_fusion.1 = f32[8,2,8,2,8,16,8]{5,6,3,1,4,2,0:T(8,128)} fusion(f32[16,8,8,8,8,1,1]{0,4,6,5,3,2,1:T(8,128)S(1)} %bitcast.148, f32[2,2,16]{2,1,0:T(2,128)} %copy-done.41, s32[2,2,16]{2,1,0:T(2,128)} %copy-done.44), kind=kOutput, calls=%fused_computation.1 | convolution fusion | flops 50333696 | bytes 1311232 | tf_op jit(solution)/shard_map/sxyz,slijk->lxiyjzk/dot_general | solution.py:108
  71.7 12.3 %copy.25 = f32[8,2,8,2,8,16,8]{6,5,4,3,2,1,0:T(8,128)} copy(f32[8,2,8,2,8,16,8]{5,6,3,1,4,2,0:T(8,128)} %convolution_bitcast_fusion.1) | data formatting | bytes 2097152 | tf_op jit(solution)/shard_map/sxyz,slijk->lxiyjzk/transpose | solution.py:108
  84.0 11.8 %reshape.119 = f32[8,16,16,128]{3,2,1,0:T(8,128)S(1)} reshape(f32[8,2,8,2,8,16,8]{6,5,4,3,2,1,0:T(8,128)} %copy.25) | data formatting | bytes 2097152 | tf_op jit(solution)/shard_map/reshape | solution.py:111
  98.0 4.5 collective-permute-start.1
  105.0 2.1 collective-permute-start.5
  107.2 2.2 collective-permute-start.7
  113.2 2.4 fusion.112
  115.5 2.4 copy.28
  117.9 2.7 collective-permute-start.11
  120.7 2.4 copy.26
  123.1 3.1 collective-permute-start.9
  128.1 2.2 copy.29
  130.3 2.2 copy.27
  132.5 5.9 %multiply_reduce_fusion.1 = (f32[8]{0:T(128)}, f32[8]{0:T(128)}, f32[8,16,16,128]{3,2,1,0:T(8,128)S(1)}) fusion(f32[8,16,16,128]{3,2,1,0:T(8,128)S(1)} %reshape.119, f32[8,16,16,128]{3,2,1,0:T(8,128)S(1)} %copy-done.1, f32[16,16,128]{2,1,0:T(8,128)S(1)} %mul.300, f32[8,18,1,128]{3,2,1,0:T(1,128)} %copy-done.33, f32[8,18,16,128]{3,2,1,0:T(8,128)} %copy-done.7, ...), kind=kLoop, calls=%fused_computation.104 | loop fusion | flops 8912880 | bytes 5673280 | tf_op jit(solution)/shard_map/reduce_sum | solution.py:45
  138.4 42.6 %all-reduce.1 = (f32[8]{0:T(128)}, f32[8]{0:T(128)}) all-reduce(f32[8]{0:T(128)} %get-tuple-element.10, f32[8]{0:T(128)} %get-tuple-element.9), channel_id=1, replica_groups=mesh['span'=2,'height'=4,'depth'=4] {'span','height','depth'}, use_global_device_ids=true, to_apply=%region_3.4 | all-reduce | flops 16 | bytes 128 | tf_op jit(solution)/shard_map/psum | solution.py:49
  183.2 11.9 %reshape.121 = bf16[8,2,8,2,8,16,8]{6,5,4,3,2,1,0:T(8,128)(2,1)} reshape(bf16[8,16,16,128]{3,2,1,0:T(8,128)(2,1)} %fusion.87) | data formatting | bytes 1048576 | tf_op jit(solution)/shard_map/reshape | solution.py:97
  195.1 6.2 %bitcast_convert_fusion = bf16[16,8,8,8,8]{0,4,3,2,1:T(8,128)(2,1)S(1)} fusion(bf16[8,2,8,2,8,16,8]{6,5,4,3,2,1,0:T(8,128)(2,1)} %reshape.121, f32[2,2,16]{2,1,0:T(2,128)} %copy-done.41, s32[2,2,16]{2,1,0:T(2,128)} %copy-done.44), kind=kOutput, calls=%fused_computation.2 | convolution fusion | flops 8456192 | bytes 655872 | tf_op jit(solution)/shard_map/sxyz,lxiyjzk->slijk/dot_general | solution.py:100
  201.7 5.5 %all_to_all.20 = bf16[16,8,512]{2,1,0:T(8,128)(2,1)S(1)} all-to-all(bf16[16,8,512]{2,1,0:T(8,128)(2,1)S(1)} %copy.31), channel_id=1, replica_groups=mesh['span'=2,'height'=4,'depth'=4] {'span'}, dimensions={0} | all-to-all | bytes 262144 | tf_op jit(solution)/shard_map/all_to_all | solution.py:105
  207.3 5.6 %fusion.124 = f32[16,8,512]{2,1,0:T(8,128)S(1)} fusion(bf16[16,8,512]{2,1,0:T(8,128)(2,1)S(1)} %all_to_all.20, bf16[16,512,512]{2,1,0:T(8,128)(2,1)} %param.9), kind=kOutput, calls=%fused_computation.251 | convolution fusion | flops 67108864 | bytes 8781824 | tf_op jit(solution)/shard_map/sij,slj->sli/dot_general | solution.py:93
  212.9 7.7 %all_to_all.21 = f32[16,8,512]{2,1,0:T(8,128)S(1)} all-to-all(f32[16,8,512]{2,1,0:T(8,128)S(1)} %fusion.124), channel_id=1, replica_groups=mesh['span'=2,'height'=4,'depth'=4] {'span'}, dimensions={0} | all-to-all | bytes 524288 | tf_op jit(solution)/shard_map/all_to_all | solution.py:94
  222.5 10.1 %convolution_bitcast_fusion = f32[8,2,8,2,8,16,8]{5,6,3,1,4,2,0:T(8,128)} fusion(f32[16,8,8,8,8,1,1]{0,4,6,5,3,2,1:T(8,128)} %bitcast.147, f32[2,2,16]{2,1,0:T(2,128)S(1)} %copy-done.43, s32[2,2,16]{2,1,0:T(2,128)S(1)} %copy-done.45), kind=kOutput, calls=%fused_computation | convolution fusion | flops 50333696 | bytes 1311232 | tf_op jit(solution)/shard_map/sxyz,slijk->lxiyjzk/dot_general | solution.py:108
  232.6 12.3 %copy.33 = f32[8,2,8,2,8,16,8]{6,5,4,3,2,1,0:T(8,128)} copy(f32[8,2,8,2,8,16,8]{5,6,3,1,4,2,0:T(8,128)} %convolution_bitcast_fusion) | data formatting | bytes 2097152 | tf_op jit(solution)/shard_map/sxyz,slijk->lxiyjzk/transpose | solution.py:108
  244.9 11.9 %reshape.124 = f32[8,16,16,128]{3,2,1,0:T(8,128)S(1)} reshape(f32[8,2,8,2,8,16,8]{6,5,4,3,2,1,0:T(8,128)} %copy.33) | data formatting | bytes 2097152 | tf_op jit(solution)/shard_map/reshape | solution.py:111
  258.8 4.5 collective-permute-start.25
  264.7 4.8 %collective-permute-start.12 = (f32[8,1,16,128]{3,2,1,0:T(8,128)S(1)}, f32[8,1,16,128]{3,2,1,0:T(8,128)S(1)}, u32[]{:S(2)}, u32[]{:S(2)}) collective-permute-start(f32[8,1,16,128]{3,2,1,0:T(8,128)S(1)} %get-tuple-element.34), channel_id=1, source_target_pairs={{16,0},{17,1},{18,2},{19,3},{20,4},{21,5},{22,6},{23,7},{24,8},{25... | collective-permute-start | bytes 196616 | tf_op jit(solution)/shard_map/ppermute | solution.py:24
  270.1 2.2 constant_dynamic-update-slice_fusion.4
  274.3 2.4 collective-permute-start.15
  276.8 3.2 collective-permute-start.27
  282.9 2.4 fusion.111
  285.3 3.1 copy.36
  288.3 3.3 collective-permute-start.17
  291.6 3.0 copy.34
  294.6 3.2 collective-permute-start.16
  298.6 3.1 copy.37
  301.8 3.1 copy.35
  304.9 5.0 %fusion.22 = f32[8]{0:T(128)S(1)} fusion(f32[8,16,16,128]{3,2,1,0:T(8,128)S(1)} %reshape.124, f32[8,18,18,1]{3,2,1,0:T(8,128)} %copy.37, f32[8,18,1,128]{3,2,1,0:T(1,128)S(1)} %collective-permute-done.14, f32[8,18,16,128]{3,2,1,0:T(8,128)} %copy-done.8, f32[8,18,1,128]{3,2,1,0:T(1,128)} %copy-done.35, f32[8,18,18,1]{3,2,1,0:T(8,128)} %copy.35, ...), kind=kLoop, calls=%fused_computation.48 | loop fusion | flops 8126456 | bytes 3445024 | tf_op jit(solution)/shard_map/reduce_sum | solution.py:45
  310.0 39.8 %all-reduce = (f32[8]{0:T(128)S(1)}, f32[8]{0:T(128)S(1)}) all-reduce(f32[8]{0:T(128)S(1)} %copy-done.59, f32[8]{0:T(128)S(1)} %fusion.22), channel_id=1, replica_groups=mesh['span'=2,'height'=4,'depth'=4] {'span','height','depth'}, use_global_device_ids=true, to_apply=%region_7.8 | all-reduce | flops 16 | bytes 128 | tf_op jit(solution)/shard_map/psum | solution.py:49
  350.8 2.9 collective-permute-start.18
  356.1 3.3 collective-permute-start.29
  359.3 2.6 collective-permute-start.28
  364.0 2.4 collective-permute-start.21
  367.5 2.2 collective-permute-done.21
  371.7 3.0 copy.38
  374.7 3.3 collective-permute-start.22
  379.6 2.6 collective-permute-start.23
  386.0 2.2 copy.41
  388.2 3.2 fusion.5
  393.5 41.7 %pmax.7 = f32[]{:T(128)} all-reduce(f32[]{:T(128)} %get-tuple-element.15), channel_id=1, replica_groups=mesh['span'=2,'height'=4,'depth'=4] {'span','height','depth'}, use_global_device_ids=true, to_apply=%region_17.18 | all-reduce | flops 1 | bytes 8 | tf_op jit(solution)/shard_map/pmax | solution.py:143
  439.2 4.2 collective-permute-done.30
  445.3 2.4 collective-permute-start.32
  447.8 2.6 collective-permute-done.32
  450.5 3.2 collective-permute-start.35
  453.7 2.6 collective-permute-start.34
  457.1 3.2 collective-permute-done.34
  (229 shorter events, 61.2 us)
Async XLA Ops:
  5.8 15.1 %collective-permute-start = (f32[2,1,16,128]{3,2,1,0:T(8,128)S(1)}, f32[2,1,16,128]{3,2,1,0:T(8,128)S(1)}, u32[]{:S(2)}, u32[]{:S(2)}) collective-permute-start(f32[2,1,16,128]{3,2,1,0:T(8,128)S(1)} %get-tuple-element.49), channel_id=1, source_target_pairs={{16,0},{17,1},{18,2},{19,3},{20,4},{21,5},{22,6},{23,7},{24,8},{25... | collective-permute-start | bytes 49160 | tf_op jit(solution)/shard_map/ppermute | solution.py:24
  8.2 12.6 %collective-permute-start.2 = (f32[2,1,16,128]{3,2,1,0:T(8,128)S(1)}, f32[2,1,16,128]{3,2,1,0:T(8,128)S(1)}, u32[]{:S(2)}, u32[]{:S(2)}) collective-permute-start(f32[2,1,16,128]{3,2,1,0:T(8,128)S(1)} %get-tuple-element.48), channel_id=1, source_target_pairs={{0,16},{1,17},{2,18},{3,19},{4,20},{5,21},{6,22},{7,23},{8,24},{9,... | collective-permute-start | bytes 49160 | tf_op jit(solution)/shard_map/ppermute | solution.py:21
  10.2 15.0 %copy-start.44 = (s32[2,2,16]{2,1,0:T(2,128)}, s32[2,2,16]{2,1,0:T(2,128)S(1)}, u32[]{:S(2)}) copy-start(s32[2,2,16]{2,1,0:T(2,128)S(1)} %multiply_add_fusion.1) | copy-start | bytes 772
  10.2 15.0 %copy-start.42 = (f32[2,2,16]{2,1,0:T(2,128)S(1)}, f32[2,2,16]{2,1,0:T(2,128)}, u32[]{:S(2)}) copy-start(f32[2,2,16]{2,1,0:T(2,128)} %copy-done.41) | copy-start | bytes 772
  20.8 36.5 %copy-start.21 = (f32[2,1,16,128]{3,2,1,0:T(8,128)}, f32[2,1,16,128]{3,2,1,0:T(8,128)S(1)}, u32[]{:S(2)}) copy-start(f32[2,1,16,128]{3,2,1,0:T(8,128)S(1)} %collective-permute-done.2) | copy-start | bytes 49156
  20.9 17.6 %collective-permute-start.4 = (f32[2,18,1,128]{3,2,1,0:T(1,128)S(1)}, f32[2,18,1,128]{3,2,1,0:T(1,128)S(1)}, u32[]{:S(2)}, u32[]{:S(2)}) collective-permute-start(f32[2,18,1,128]{3,2,1,0:T(1,128)S(1)} %get-tuple-element.47), channel_id=1, source_target_pairs={{4,0},{8,4},{12,8},{5,1},{9,5},{13,9},{6,2},{10,6},{14,10},{7,3},{... | collective-permute-start | bytes 55304 | tf_op jit(solution)/shard_map/ppermute | solution.py:24
  22.8 15.7 %collective-permute-start.6 = (f32[2,18,1,128]{3,2,1,0:T(1,128)S(1)}, f32[2,18,1,128]{3,2,1,0:T(1,128)S(1)}, u32[]{:S(2)}, u32[]{:S(2)}) collective-permute-start(f32[2,18,1,128]{3,2,1,0:T(1,128)S(1)} %get-tuple-element.46), channel_id=1, source_target_pairs={{0,4},{4,8},{8,12},{1,5},{5,9},{9,13},{2,6},{6,10},{10,14},{3,7},{... | collective-permute-start | bytes 55304 | tf_op jit(solution)/shard_map/ppermute | solution.py:21
  32.5 13.9 %all-to-all-start = ((bf16[16,8,512]{2,1,0:T(8,128)(2,1)}), bf16[16,8,512]{2,1,0:T(8,128)(2,1)S(1)}, u32[]{:S(2)}, u32[]{:S(2)}) async-start(bf16[16,8,512]{2,1,0:T(8,128)(2,1)} %copy.23), calls=%async_computation | async-start | bytes 262144 | tf_op jit(solution)/shard_map/all_to_all | solution.py:105
  38.5 14.2 %copy-start.27 = (f32[2,18,1,128]{3,2,1,0:T(1,128)}, f32[2,18,1,128]{3,2,1,0:T(1,128)S(1)}, u32[]{:S(2)}) copy-start(f32[2,18,1,128]{3,2,1,0:T(1,128)S(1)} %collective-permute-done.4) | copy-start | bytes 55300
  38.5 18.8 %copy-start.30 = (f32[2,18,1,128]{3,2,1,0:T(1,128)}, f32[2,18,1,128]{3,2,1,0:T(1,128)S(1)}, u32[]{:S(2)}) copy-start(f32[2,18,1,128]{3,2,1,0:T(1,128)S(1)} %collective-permute-done.6) | copy-start | bytes 55300
  39.6 69.8 %collective-permute-start.10 = (f32[2,18,18,1]{3,2,1,0:T(8,128)}, f32[2,18,18,1]{3,2,1,0:T(8,128)}, u32[]{:S(2)}, u32[]{:S(2)}) collective-permute-start(f32[2,18,18,1]{3,2,1,0:T(8,128)} %get-tuple-element.45), channel_id=1, source_target_pairs={{0,1},{1,2},{2,3},{4,5},{5,6},{6,7},{8,9},{9,10},{10,11},{12,13},{... | collective-permute-start | bytes 7784 | tf_op jit(solution)/shard_map/ppermute | solution.py:21
  43.1 14.2 %copy-start.4 = (f32[16,16,128]{2,1,0:T(8,128)S(1)}, f32[16,16,128]{2,1,0:T(8,128)}, u32[]{:S(2)}) copy-start(f32[16,16,128]{2,1,0:T(8,128)} %param.6) | copy-start | bytes 393220
  43.1 83.1 %collective-permute-start.8 = (f32[2,18,18,1]{3,2,1,0:T(8,128)}, f32[2,18,18,1]{3,2,1,0:T(8,128)}, u32[]{:S(2)}, u32[]{:S(2)}) collective-permute-start(f32[2,18,18,1]{3,2,1,0:T(8,128)} %get-tuple-element.44), channel_id=1, source_target_pairs={{1,0},{2,1},{3,2},{5,4},{6,5},{7,6},{9,8},{10,9},{11,10},{13,12},{... | collective-permute-start | bytes 7784 | tf_op jit(solution)/shard_map/ppermute | solution.py:24
  52.7 7.9 %all-to-all-start.1 = ((f32[16,8,512]{2,1,0:T(8,128)}), f32[16,8,512]{2,1,0:T(8,128)}, u32[]{:S(2)}, u32[]{:S(2)}) async-start(f32[16,8,512]{2,1,0:T(8,128)} %fusion.123), calls=%async_computation.1 | async-start | bytes 524288 | tf_op jit(solution)/shard_map/all_to_all | solution.py:94
  84.0 13.1 %copy-start.5 = (f32[16,16,128]{2,1,0:T(8,128)S(1)}, f32[16,16,128]{2,1,0:T(8,128)}, u32[]{:S(2)}) copy-start(f32[16,16,128]{2,1,0:T(8,128)} %param.6) | copy-start | bytes 393220
  84.0 13.2 %copy-start.22 = (f32[2,1,16,128]{3,2,1,0:T(8,128)S(1)}, f32[2,1,16,128]{3,2,1,0:T(8,128)}, u32[]{:S(2)}) copy-start(f32[2,1,16,128]{3,2,1,0:T(8,128)} %copy-done.21) | copy-start | bytes 49156
  84.0 13.2 %copy-start.28 = (f32[2,18,1,128]{3,2,1,0:T(1,128)S(1)}, f32[2,18,1,128]{3,2,1,0:T(1,128)}, u32[]{:S(2)}) copy-start(f32[2,18,1,128]{3,2,1,0:T(1,128)} %copy-done.27) | copy-start | bytes 55300
  95.9 13.5 %copy-start.31 = (f32[2,18,1,128]{3,2,1,0:T(1,128)S(1)}, f32[2,18,1,128]{3,2,1,0:T(1,128)}, u32[]{:S(2)}) copy-start(f32[2,18,1,128]{3,2,1,0:T(1,128)} %copy-done.30) | copy-start | bytes 55300
  95.9 6.7 %collective-permute-start.3 = (f32[8,1,16,128]{3,2,1,0:T(8,128)S(1)}, f32[8,1,16,128]{3,2,1,0:T(8,128)S(1)}, u32[]{:S(2)}, u32[]{:S(2)}) collective-permute-start(f32[8,1,16,128]{3,2,1,0:T(8,128)S(1)} %get-tuple-element.39), channel_id=1, source_target_pairs={{0,16},{1,17},{2,18},{3,19},{4,20},{5,21},{6,22},{7,23},{8,24},{9,... | collective-permute-start | bytes 196616 | tf_op jit(solution)/shard_map/ppermute | solution.py:21
  98.0 6.4 %collective-permute-start.1 = (f32[8,1,16,128]{3,2,1,0:T(8,128)S(1)}, f32[8,1,16,128]{3,2,1,0:T(8,128)S(1)}, u32[]{:S(2)}, u32[]{:S(2)}) collective-permute-start(f32[8,1,16,128]{3,2,1,0:T(8,128)S(1)} %get-tuple-element.38), channel_id=1, source_target_pairs={{16,0},{17,1},{18,2},{19,3},{20,4},{21,5},{22,6},{23,7},{24,8},{25... | collective-permute-start | bytes 196616 | tf_op jit(solution)/shard_map/ppermute | solution.py:24
  105.0 6.2 %collective-permute-start.5 = (f32[8,18,1,128]{3,2,1,0:T(1,128)S(1)}, f32[8,18,1,128]{3,2,1,0:T(1,128)S(1)}, u32[]{:S(2)}, u32[]{:S(2)}) collective-permute-start(f32[8,18,1,128]{3,2,1,0:T(1,128)S(1)} %get-tuple-element.31), channel_id=1, source_target_pairs={{4,0},{8,4},{12,8},{5,1},{9,5},{13,9},{6,2},{10,6},{14,10},{7,3},{... | collective-permute-start | bytes 221192 | tf_op jit(solution)/shard_map/ppermute | solution.py:24
  107.2 5.7 %collective-permute-start.7 = (f32[8,18,1,128]{3,2,1,0:T(1,128)S(1)}, f32[8,18,1,128]{3,2,1,0:T(1,128)S(1)}, u32[]{:S(2)}, u32[]{:S(2)}) collective-permute-start(f32[8,18,1,128]{3,2,1,0:T(1,128)S(1)} %get-tuple-element.30), channel_id=1, source_target_pairs={{0,4},{4,8},{8,12},{1,5},{5,9},{9,13},{2,6},{6,10},{10,14},{3,7},{... | collective-permute-start | bytes 221192 | tf_op jit(solution)/shard_map/ppermute | solution.py:21
  117.9 10.2 %collective-permute-start.11 = (f32[8,18,18,1]{2,0,3,1:T(8,128)S(1)}, f32[8,18,18,1]{2,0,3,1:T(8,128)S(1)}, u32[]{:S(2)}, u32[]{:S(2)}) collective-permute-start(f32[8,18,18,1]{2,0,3,1:T(8,128)S(1)} %copy.28), channel_id=1, source_target_pairs={{0,1},{1,2},{2,3},{4,5},{5,6},{6,7},{8,9},{9,10},{10,11},{12,13},{... | collective-permute-start | bytes 31112 | tf_op jit(solution)/shard_map/ppermute | solution.py:21
  123.1 7.2 %collective-permute-start.9 = (f32[8,18,18,1]{2,0,3,1:T(8,128)S(1)}, f32[8,18,18,1]{2,0,3,1:T(8,128)S(1)}, u32[]{:S(2)}, u32[]{:S(2)}) collective-permute-start(f32[8,18,18,1]{2,0,3,1:T(8,128)S(1)} %copy.26), channel_id=1, source_target_pairs={{1,0},{2,1},{3,2},{5,4},{6,5},{7,6},{9,8},{10,9},{11,10},{13,12},{... | collective-permute-start | bytes 31112 | tf_op jit(solution)/shard_map/ppermute | solution.py:24
  138.4 56.8 %copy-start.3 = (f32[8,16,16,128]{3,2,1,0:T(8,128)}, f32[8,16,16,128]{3,2,1,0:T(8,128)S(1)}, u32[]{:S(2)}) copy-start(f32[8,16,16,128]{3,2,1,0:T(8,128)S(1)} %get-tuple-element.19) | copy-start | bytes 3145732
  244.9 25.1 %copy-start.2 = (f32[8,16,16,128]{3,2,1,0:T(8,128)S(1)}, f32[8,16,16,128]{3,2,1,0:T(8,128)}, u32[]{:S(2)}) copy-start(f32[8,16,16,128]{3,2,1,0:T(8,128)} %param.5) | copy-start | bytes 3145732
  256.8 12.6 %collective-permute-start.13 = (f32[8,1,16,128]{3,2,1,0:T(8,128)S(1)}, f32[8,1,16,128]{3,2,1,0:T(8,128)S(1)}, u32[]{:S(2)}, u32[]{:S(2)}) collective-permute-start(f32[8,1,16,128]{3,2,1,0:T(8,128)S(1)} %get-tuple-element.35), channel_id=1, source_target_pairs={{0,16},{1,17},{2,18},{3,19},{4,20},{5,21},{6,22},{7,23},{8,24},{9,... | collective-permute-start | bytes 196616 | tf_op jit(solution)/shard_map/ppermute | solution.py:21
  258.8 17.9 %collective-permute-start.25 = (bf16[1,16,128]{2,1,0:T(8,128)(2,1)S(1)}, bf16[1,16,128]{2,1,0:T(8,128)(2,1)S(1)}, u32[]{:S(2)}, u32[]{:S(2)}) collective-permute-start(bf16[1,16,128]{2,1,0:T(8,128)(2,1)S(1)} %get-tuple-element.63), channel_id=1, source_target_pairs={{16,0},{17,1},{18,2},{19,3},{20,4},{21,5},{22,6},{23,7},{24,8},{25... | collective-permute-start | bytes 12296 | tf_op jit(solution)/shard_map/ppermute | solution.py:24
  263.4 13.4 %collective-permute-start.24 = (bf16[1,16,128]{2,1,0:T(8,128)(2,1)S(1)}, bf16[1,16,128]{2,1,0:T(8,128)(2,1)S(1)}, u32[]{:S(2)}, u32[]{:S(2)}) collective-permute-start(bf16[1,16,128]{2,1,0:T(8,128)(2,1)S(1)} %get-tuple-element.62), channel_id=1, source_target_pairs={{0,16},{1,17},{2,18},{3,19},{4,20},{5,21},{6,22},{7,23},{8,24},{9,... | collective-permute-start | bytes 12296 | tf_op jit(solution)/shard_map/ppermute | solution.py:21
  264.7 7.6 %collective-permute-start.12 = (f32[8,1,16,128]{3,2,1,0:T(8,128)S(1)}, f32[8,1,16,128]{3,2,1,0:T(8,128)S(1)}, u32[]{:S(2)}, u32[]{:S(2)}) collective-permute-start(f32[8,1,16,128]{3,2,1,0:T(8,128)S(1)} %get-tuple-element.34), channel_id=1, source_target_pairs={{16,0},{17,1},{18,2},{19,3},{20,4},{21,5},{22,6},{23,7},{24,8},{25... | collective-permute-start | bytes 196616 | tf_op jit(solution)/shard_map/ppermute | solution.py:24
  272.4 9.5 %collective-permute-start.14 = (f32[8,18,1,128]{3,2,1,0:T(1,128)S(1)}, f32[8,18,1,128]{3,2,1,0:T(1,128)S(1)}, u32[]{:S(2)}, u32[]{:S(2)}) collective-permute-start(f32[8,18,1,128]{3,2,1,0:T(1,128)S(1)} %get-tuple-element.29), channel_id=1, source_target_pairs={{4,0},{8,4},{12,8},{5,1},{9,5},{13,9},{6,2},{10,6},{14,10},{7,3},{... | collective-permute-start | bytes 221192 | tf_op jit(solution)/shard_map/ppermute | solution.py:24
  274.3 7.6 %collective-permute-start.15 = (f32[8,18,1,128]{3,2,1,0:T(1,128)S(1)}, f32[8,18,1,128]{3,2,1,0:T(1,128)S(1)}, u32[]{:S(2)}, u32[]{:S(2)}) collective-permute-start(f32[8,18,1,128]{3,2,1,0:T(1,128)S(1)} %get-tuple-element.28), channel_id=1, source_target_pairs={{0,4},{4,8},{8,12},{1,5},{5,9},{9,13},{2,6},{6,10},{10,14},{3,7},{... | collective-permute-start | bytes 221192 | tf_op jit(solution)/shard_map/ppermute | solution.py:21
  276.8 21.0 %collective-permute-start.27 = (bf16[18,1,128]{2,1,0:T(2,128)(2,1)S(1)}, bf16[18,1,128]{2,1,0:T(2,128)(2,1)S(1)}, u32[]{:S(2)}, u32[]{:S(2)}) collective-permute-start(bf16[18,1,128]{2,1,0:T(2,128)(2,1)S(1)} %get-tuple-element.59), channel_id=1, source_target_pairs={{4,0},{8,4},{12,8},{5,1},{9,5},{13,9},{6,2},{10,6},{14,10},{7,3},{... | collective-permute-start | bytes 13832 | tf_op jit(solution)/shard_map/ppermute | solution.py:24
  280.0 17.9 %collective-permute-start.26 = (bf16[18,1,128]{2,1,0:T(2,128)(2,1)S(1)}, bf16[18,1,128]{2,1,0:T(2,128)(2,1)S(1)}, u32[]{:S(2)}, u32[]{:S(2)}) collective-permute-start(bf16[18,1,128]{2,1,0:T(2,128)(2,1)S(1)} %get-tuple-element.58), channel_id=1, source_target_pairs={{0,4},{4,8},{8,12},{1,5},{5,9},{9,13},{2,6},{6,10},{10,14},{3,7},{... | collective-permute-start | bytes 13832 | tf_op jit(solution)/shard_map/ppermute | solution.py:21
  285.2 12.6 %copy-start.19 = (bf16[16,16,128]{2,1,0:T(8,128)(2,1)S(1)}, bf16[16,16,128]{2,1,0:T(8,128)(2,1)}, u32[]{:S(2)}) copy-start(bf16[16,16,128]{2,1,0:T(8,128)(2,1)} %get-tuple-element.50) | copy-start | bytes 196612
  285.2 12.6 %copy-start.47 = (bf16[1,16,128]{2,1,0:T(8,128)(2,1)S(1)}, bf16[1,16,128]{2,1,0:T(8,128)(2,1)}, u32[]{:S(2)}) copy-start(bf16[1,16,128]{2,1,0:T(8,128)(2,1)} %copy-done.46) | copy-start | bytes 12292
  285.2 12.6 %copy-start.50 = (bf16[1,16,128]{2,1,0:T(8,128)(2,1)S(1)}, bf16[1,16,128]{2,1,0:T(8,128)(2,1)}, u32[]{:S(2)}) copy-start(bf16[1,16,128]{2,1,0:T(8,128)(2,1)} %copy-done.49) | copy-start | bytes 12292
  288.3 10.3 %collective-permute-start.17 = (f32[8,18,18,1]{2,0,3,1:T(8,128)}, f32[8,18,18,1]{2,0,3,1:T(8,128)}, u32[]{:S(2)}, u32[]{:S(2)}) collective-permute-start(f32[8,18,18,1]{2,0,3,1:T(8,128)} %copy.36), channel_id=1, source_target_pairs={{0,1},{1,2},{2,3},{4,5},{5,6},{6,7},{8,9},{9,10},{10,11},{12,13},{... | collective-permute-start | bytes 31112 | tf_op jit(solution)/shard_map/ppermute | solution.py:21
  294.6 7.1 %collective-permute-start.16 = (f32[8,18,18,1]{2,0,3,1:T(8,128)}, f32[8,18,18,1]{2,0,3,1:T(8,128)}, u32[]{:S(2)}, u32[]{:S(2)}) collective-permute-start(f32[8,18,18,1]{2,0,3,1:T(8,128)} %copy.34), channel_id=1, source_target_pairs={{1,0},{2,1},{3,2},{5,4},{6,5},{7,6},{9,8},{10,9},{11,10},{13,12},{... | collective-permute-start | bytes 31112 | tf_op jit(solution)/shard_map/ppermute | solution.py:24
  304.9 44.9 %copy-start.60 = (f32[8]{0:T(128)S(1)}, f32[8]{0:T(128)}, u32[]{:S(2)}) copy-start(f32[8]{0:T(128)} %get-tuple-element.13) | copy-start | bytes 100
  304.9 44.9 %copy-start.61 = (f32[8]{0:T(128)S(1)}, f32[8]{0:T(128)}, u32[]{:S(2)}) copy-start(f32[8]{0:T(128)} %get-tuple-element.14) | copy-start | bytes 100
  350.7 37.5 %copy-start = (f32[8,16,16,128]{3,2,1,0:T(8,128)}, f32[8,16,16,128]{3,2,1,0:T(8,128)S(1)}, u32[]{:S(2)}) copy-start(f32[8,16,16,128]{3,2,1,0:T(8,128)S(1)} %multiply_add_fusion) | copy-start | bytes 3145732
  350.7 15.7 %copy-start.20 = (bf16[16,16,128]{2,1,0:T(8,128)(2,1)S(1)}, bf16[16,16,128]{2,1,0:T(8,128)(2,1)}, u32[]{:S(2)}) copy-start(bf16[16,16,128]{2,1,0:T(8,128)(2,1)} %get-tuple-element.50) | copy-start | bytes 196612
  350.8 15.7 %copy-start.48 = (bf16[1,16,128]{2,1,0:T(8,128)(2,1)S(1)}, bf16[1,16,128]{2,1,0:T(8,128)(2,1)}, u32[]{:S(2)}) copy-start(bf16[1,16,128]{2,1,0:T(8,128)(2,1)} %copy-done.46) | copy-start | bytes 12292
  350.8 15.7 %copy-start.51 = (bf16[1,16,128]{2,1,0:T(8,128)(2,1)S(1)}, bf16[1,16,128]{2,1,0:T(8,128)(2,1)}, u32[]{:S(2)}) copy-start(bf16[1,16,128]{2,1,0:T(8,128)(2,1)} %copy-done.49) | copy-start | bytes 12292
  350.8 15.7 %copy-start.53 = (bf16[18,1,128]{2,1,0:T(2,128)(2,1)S(1)}, bf16[18,1,128]{2,1,0:T(2,128)(2,1)}, u32[]{:S(2)}) copy-start(bf16[18,1,128]{2,1,0:T(2,128)(2,1)} %copy-done.52) | copy-start | bytes 13828
  350.8 15.7 %copy-start.55 = (bf16[18,1,128]{2,1,0:T(2,128)(2,1)S(1)}, bf16[18,1,128]{2,1,0:T(2,128)(2,1)}, u32[]{:S(2)}) copy-start(bf16[18,1,128]{2,1,0:T(2,128)(2,1)} %copy-done.54) | copy-start | bytes 13828
  350.8 11.1 %collective-permute-start.18 = (f32[8,1,16,128]{3,2,1,0:T(8,128)S(1)}, f32[8,1,16,128]{3,2,1,0:T(8,128)S(1)}, u32[]{:S(2)}, u32[]{:S(2)}) collective-permute-start(f32[8,1,16,128]{3,2,1,0:T(8,128)S(1)} %get-tuple-element.33), channel_id=1, source_target_pairs={{16,0},{17,1},{18,2},{19,3},{20,4},{21,5},{22,6},{23,7},{24,8},{25... | collective-permute-start | bytes 196616 | tf_op jit(solution)/shard_map/ppermute | solution.py:24
  353.7 8.2 %collective-permute-start.19 = (f32[8,1,16,128]{3,2,1,0:T(8,128)S(1)}, f32[8,1,16,128]{3,2,1,0:T(8,128)S(1)}, u32[]{:S(2)}, u32[]{:S(2)}) collective-permute-start(f32[8,1,16,128]{3,2,1,0:T(8,128)S(1)} %get-tuple-element.32), channel_id=1, source_target_pairs={{0,16},{1,17},{2,18},{3,19},{4,20},{5,21},{6,22},{7,23},{8,24},{9,... | collective-permute-start | bytes 196616 | tf_op jit(solution)/shard_map/ppermute | solution.py:21
  356.1 10.3 %collective-permute-start.29 = (bf16[18,18,1]{2,1,0:T(8,128)(2,1)S(1)}, bf16[18,18,1]{2,1,0:T(8,128)(2,1)S(1)}, u32[]{:S(2)}, u32[]{:S(2)}) collective-permute-start(bf16[18,18,1]{2,1,0:T(8,128)(2,1)S(1)} %get-tuple-element.55), channel_id=1, source_target_pairs={{1,0},{2,1},{3,2},{5,4},{6,5},{7,6},{9,8},{10,9},{11,10},{13,12},{... | collective-permute-start | bytes 1952 | tf_op jit(solution)/shard_map/ppermute | solution.py:24
  359.3 7.1 %collective-permute-start.28 = (bf16[18,18,1]{2,1,0:T(8,128)(2,1)S(1)}, bf16[18,18,1]{2,1,0:T(8,128)(2,1)S(1)}, u32[]{:S(2)}, u32[]{:S(2)}) collective-permute-start(bf16[18,18,1]{2,1,0:T(8,128)(2,1)S(1)} %get-tuple-element.54), channel_id=1, source_target_pairs={{0,1},{1,2},{2,3},{4,5},{5,6},{6,7},{8,9},{9,10},{10,11},{12,13},{... | collective-permute-start | bytes 1952 | tf_op jit(solution)/shard_map/ppermute | solution.py:21
  362.1 5.4 %collective-permute-start.20 = (f32[8,18,1,128]{3,2,1,0:T(1,128)S(1)}, f32[8,18,1,128]{3,2,1,0:T(1,128)S(1)}, u32[]{:S(2)}, u32[]{:S(2)}) collective-permute-start(f32[8,18,1,128]{3,2,1,0:T(1,128)S(1)} %get-tuple-element.27), channel_id=1, source_target_pairs={{4,0},{8,4},{12,8},{5,1},{9,5},{13,9},{6,2},{10,6},{14,10},{7,3},{... | collective-permute-start | bytes 221192 | tf_op jit(solution)/shard_map/ppermute | solution.py:24
  364.0 5.7 %collective-permute-start.21 = (f32[8,18,1,128]{3,2,1,0:T(1,128)S(1)}, f32[8,18,1,128]{3,2,1,0:T(1,128)S(1)}, u32[]{:S(2)}, u32[]{:S(2)}) collective-permute-start(f32[8,18,1,128]{3,2,1,0:T(1,128)S(1)} %get-tuple-element.26), channel_id=1, source_target_pairs={{0,4},{4,8},{8,12},{1,5},{5,9},{9,13},{2,6},{6,10},{10,14},{3,7},{... | collective-permute-start | bytes 221192 | tf_op jit(solution)/shard_map/ppermute | solution.py:21
  369.7 12.5 %copy-start.24 = (f32[8,18,1,128]{3,2,1,0:T(1,128)}, f32[8,18,1,128]{3,2,1,0:T(1,128)S(1)}, u32[]{:S(2)}) copy-start(f32[8,18,1,128]{3,2,1,0:T(1,128)S(1)} %collective-permute-done.21) | copy-start | bytes 221188
  374.7 8.4 %collective-permute-start.22 = (f32[8,18,18,1]{2,0,3,1:T(8,128)}, f32[8,18,18,1]{2,0,3,1:T(8,128)}, u32[]{:S(2)}, u32[]{:S(2)}) collective-permute-start(f32[8,18,18,1]{2,0,3,1:T(8,128)} %copy.38), channel_id=1, source_target_pairs={{1,0},{2,1},{3,2},{5,4},{6,5},{7,6},{9,8},{10,9},{11,10},{13,12},{... | collective-permute-start | bytes 31112 | tf_op jit(solution)/shard_map/ppermute | solution.py:24
  379.6 6.4 %collective-permute-start.23 = (f32[8,18,18,1]{2,0,3,1:T(8,128)}, f32[8,18,18,1]{2,0,3,1:T(8,128)S(1)}, u32[]{:S(2)}, u32[]{:S(2)}) collective-permute-start(f32[8,18,18,1]{2,0,3,1:T(8,128)} %copy.40), channel_id=1, source_target_pairs={{0,1},{1,2},{2,3},{4,5},{5,6},{6,7},{8,9},{9,10},{10,11},{12,13},{... | collective-permute-start | bytes 31112 | tf_op jit(solution)/shard_map/ppermute | solution.py:21
  391.5 44.4 %copy-start.9 = (f32[18,18,130]{2,1,0:T(8,128)S(1)}, f32[18,18,130]{2,1,0:T(8,128)}, u32[]{:S(2)}) copy-start(f32[18,18,130]{2,1,0:T(8,128)} %maximum_convert_fusion) | copy-start | bytes 505444
  393.5 68.0 %copy-start.17 = (f32[16,16,128]{2,1,0:T(8,128)}, f32[16,16,128]{2,1,0:T(8,128)S(1)}, u32[]{:S(2)}) copy-start(f32[16,16,128]{2,1,0:T(8,128)S(1)} %get-tuple-element.16) | copy-start | bytes 393220
  436.1 3.1 collective-permute-start.31
  437.9 5.5 %collective-permute-start.30 = (bf16[1,16,128]{2,1,0:T(8,128)(2,1)S(1)}, bf16[1,16,128]{2,1,0:T(8,128)(2,1)S(1)}, u32[]{:S(2)}, u32[]{:S(2)}) collective-permute-start(bf16[1,16,128]{2,1,0:T(8,128)(2,1)S(1)} %get-tuple-element.60), channel_id=1, source_target_pairs={{0,16},{1,17},{2,18},{3,19},{4,20},{5,21},{6,22},{7,23},{8,24},{9,... | collective-permute-start | bytes 12296 | tf_op jit(solution)/shard_map/ppermute | solution.py:21
  443.4 4.3 collective-permute-start.33
  445.3 5.0 %collective-permute-start.32 = (bf16[18,1,128]{2,1,0:T(2,128)(2,1)S(1)}, bf16[18,1,128]{2,1,0:T(2,128)(2,1)S(1)}, u32[]{:S(2)}, u32[]{:S(2)}) collective-permute-start(bf16[18,1,128]{2,1,0:T(2,128)(2,1)S(1)} %get-tuple-element.56), channel_id=1, source_target_pairs={{0,4},{4,8},{8,12},{1,5},{5,9},{9,13},{2,6},{6,10},{10,14},{3,7},{... | collective-permute-start | bytes 13832 | tf_op jit(solution)/shard_map/ppermute | solution.py:21
  450.5 6.6 %collective-permute-start.35 = (bf16[18,18,1]{2,1,0:T(8,128)(2,1)S(1)}, bf16[18,18,1]{2,1,0:T(8,128)(2,1)S(1)}, u32[]{:S(2)}, u32[]{:S(2)}) collective-permute-start(bf16[18,18,1]{2,1,0:T(8,128)(2,1)S(1)} %get-tuple-element.53), channel_id=1, source_target_pairs={{1,0},{2,1},{3,2},{5,4},{6,5},{7,6},{9,8},{10,9},{11,10},{13,12},{... | collective-permute-start | bytes 1952 | tf_op jit(solution)/shard_map/ppermute | solution.py:24
  453.7 6.6 %collective-permute-start.34 = (bf16[18,18,1]{2,1,0:T(8,128)(2,1)S(1)}, bf16[18,18,1]{2,1,0:T(8,128)(2,1)S(1)}, u32[]{:S(2)}, u32[]{:S(2)}) collective-permute-start(bf16[18,18,1]{2,1,0:T(8,128)(2,1)S(1)} %get-tuple-element.52), channel_id=1, source_target_pairs={{0,1},{1,2},{2,3},{4,5},{5,6},{6,7},{8,9},{9,10},{10,11},{12,13},{... | collective-permute-start | bytes 1952 | tf_op jit(solution)/shard_map/ppermute | solution.py:21
  (36 other events, 176.6 us)
where the time goes:
time: 471 us; the launch traced here: 462 us
  blocking collectives  137 us (29%)
  local copies, waits for them, and re-layouts  121 us (26%)
  starting transfers between devices  102 us (22%)
  matrix products  44 us (9%)
  other arithmetic  34.2 us (7%)
  waiting for transfers between devices  19.7 us (4%)
    psum x2, blocking collectives, paired_sums(): lax.psum((cell_sums(residual, search), cell_sums(image, search)), ('span'...  82.4 us
    ppermute x18, starting transfers between devices, padded_2(): lax.ppermute(lax.slice_in_dim(block, 0, width, axis=dim), axis, backward)  53.1 us
    pmax x1, blocking collectives, local(): peak_value = lax.pmax(jnp.max(-sensitivity), ('span', 'height', 'depth'))  41.7 us
    ppermute x18, starting transfers between devices, padded_2(): lax.ppermute(lax.slice_in_dim(block, block.shape[dim] - width, None, axis...  38.7 us
    transpose x2, local copies, waits for them, and re-layouts, precondition(): jnp.einsum('sxyz,slijk->lxiyjzk', selector, shaped, precision=lax.Precisi...  24.7 us
    reshape x2, local copies, waits for them, and re-layouts, precondition(): return placed.reshape(loads, extents[0], extents[1], extents[2])  23.7 us
    reshape x2, local copies, waits for them, and re-layouts, precondition(): residual.astype(jnp.bfloat16)  22.5 us
    dot_general x2, matrix products, precondition(): jnp.einsum('sxyz,slijk->lxiyjzk', selector, shaped, precision=lax.Precisi...  19.6 us
  transfers between devices with their start and end apart: 38, of which 9 were waited for; matrix products, arithmetic and copies ran while one was open for 21% of the time, Pallas kernels for 0%

commit v1 on v0

--- a/solution.py
+++ b/solution.py
@@ -2,6 +2,7 @@
 import jax.numpy as jnp
 from jax import lax
 from jax.sharding import PartitionSpec as P
+from jax.lax import psum
 
 BE = 8
 ITERS = 2
@@ -11,6 +12,7 @@
 time_step = 0.5
 interface_weight = 0.5
 epsilon_peak = 1e-06
+fill_the_slabs = lambda xin, which_axis, along_axis: psum(psum(xin, which_axis), along_axis)
 
 
 def padded_2(block, sides, width):
@@ -46,8 +48,8 @@
 
 
 def paired_sums(residual, search, image):
-    return lax.psum(
-        (cell_sums(residual, search), cell_sums(image, search)), ("span", "height", "depth")
+    return fill_the_slabs(
+        (cell_sums(residual, search), cell_sums(image, search)), ("height", "depth"), "span"
     )
 
 

time: 471 us -> 463 us (0.983)
  blocking collectives: 137 us -> 128 us
    psum x2 -> x4, blocking collectives: 82.4 us -> 72.3 us  [the longest x2 61.3 us: psum(xin, which_axis)]
  transfers between devices with their start and end apart: 38 -> 38, of which waited for: 9 -> 9; matrix products, arithmetic and copies ran while one was open for 21% -> 22% of each run, Pallas kernels for 0% -> 0%
where the time goes in v1:
time: 463 us; the launch traced here: 454 us
  blocking collectives  128 us (28%)
  local copies, waits for them, and re-layouts  121 us (26%)
  starting transfers between devices  103 us (22%)
  matrix products  44 us (10%)
  other arithmetic  34.2 us (7%)
  waiting for transfers between devices  20.1 us (4%)
    psum x2, blocking collectives, psum(xin, which_axis)  61.3 us
    ppermute x18, starting transfers between devices, padded_2(): lax.ppermute(lax.slice_in_dim(block, 0, width, axis=dim), axis, backward)  54.7 us
    pmax x1, blocking collectives, local(): peak_value = lax.pmax(jnp.max(-sensitivity), ('span', 'height', 'depth'))  41.3 us
    ppermute x18, starting transfers between devices, padded_2(): lax.ppermute(lax.slice_in_dim(block, block.shape[dim] - width, None, axis...  37.7 us
    transpose x2, local copies, waits for them, and re-layouts, precondition(): jnp.einsum('sxyz,slijk->lxiyjzk', selector, shaped, precision=lax.Precisi...  24.7 us
    reshape x2, local copies, waits for them, and re-layouts, precondition(): return placed.reshape(loads, extents[0], extents[1], extents[2])  23.7 us
    reshape x2, local copies, waits for them, and re-layouts, precondition(): residual.astype(jnp.bfloat16)  22.5 us
    dot_general x2, matrix products, precondition(): jnp.einsum('sxyz,slijk->lxiyjzk', selector, shaped, precision=lax.Precisi...  19.6 us
  transfers between devices with their start and end apart: 38, of which 9 were waited for; matrix products, arithmetic and copies ran while one was open for 22% of the time, Pallas kernels for 0%

profile of v1, /device:TPU:14, one launch (start us, length us, event | category | flops | bytes accessed | tf_op | source)
XLA Modules:
  0.0 453.5 jit_solution(16156356507478658724)
XLA Ops:
  5.8 2.4 collective-permute-start
  10.2 10.6 %reshape.116 = bf16[8,2,8,2,8,16,8]{6,5,4,3,2,1,0:T(8,128)(2,1)} reshape(bf16[8,16,16,128]{3,2,1,0:T(8,128)(2,1)S(1)} %multiply_convert_fusion) | data formatting | bytes 1048576 | tf_op jit(solution)/shard_map/reshape | solution.py:99
  22.8 2.4 collective-permute-start.6
  25.2 6.2 %bitcast_convert_fusion.1 = bf16[16,8,8,8,8]{0,4,3,2,1:T(8,128)(2,1)S(1)} fusion(bf16[8,2,8,2,8,16,8]{6,5,4,3,2,1,0:T(8,128)(2,1)} %reshape.116, f32[2,2,16]{2,1,0:T(2,128)S(1)} %copy-done.42, s32[2,2,16]{2,1,0:T(2,128)S(1)} %multiply_add_fusion.1), kind=kOutput, calls=%fused_computation.3 | convolution fusion | flops 8456192 | bytes 655872 | tf_op jit(solution)/shard_map/sxyz,lxiyjzk->slijk/dot_general | solution.py:102
  32.5 6.0 %all-to-all-start = ((bf16[16,8,512]{2,1,0:T(8,128)(2,1)}), bf16[16,8,512]{2,1,0:T(8,128)(2,1)S(1)}, u32[]{:S(2)}, u32[]{:S(2)}) async-start(bf16[16,8,512]{2,1,0:T(8,128)(2,1)} %copy.23), calls=%async_computation | async-start | bytes 262144 | tf_op jit(solution)/shard_map/all_to_all | solution.py:107
  39.6 3.5 collective-permute-start.10
  43.1 3.2 collective-permute-start.8
  46.4 6.4 %fusion.123 = f32[16,8,512]{2,1,0:T(8,128)} fusion(bf16[16,8,512]{2,1,0:T(8,128)(2,1)S(1)} %all-to-all-done, bf16[16,512,512]{2,1,0:T(8,128)(2,1)} %param.9), kind=kOutput, calls=%fused_computation.250 | convolution fusion | flops 67108864 | bytes 8781824 | tf_op jit(solution)/shard_map/sij,slj->sli/dot_general | solution.py:95
  52.7 4.6 %all-to-all-start.1 = ((f32[16,8,512]{2,1,0:T(8,128)}), f32[16,8,512]{2,1,0:T(8,128)}, u32[]{:S(2)}, u32[]{:S(2)}) async-start(f32[16,8,512]{2,1,0:T(8,128)} %fusion.123), calls=%async_computation.1 | async-start | bytes 524288 | tf_op jit(solution)/shard_map/all_to_all | solution.py:96
  58.2 2.4 all-to-all-done.1
  62.2 9.5 %convolution_bitcast_fusion.1 = f32[8,2,8,2,8,16,8]{5,6,3,1,4,2,0:T(8,128)} fusion(f32[16,8,8,8,8,1,1]{0,4,6,5,3,2,1:T(8,128)S(1)} %bitcast.148, f32[2,2,16]{2,1,0:T(2,128)} %copy-done.41, s32[2,2,16]{2,1,0:T(2,128)} %copy-done.44), kind=kOutput, calls=%fused_computation.1 | convolution fusion | flops 50333696 | bytes 1311232 | tf_op jit(solution)/shard_map/sxyz,slijk->lxiyjzk/dot_general | solution.py:110
  71.7 12.3 %copy.25 = f32[8,2,8,2,8,16,8]{6,5,4,3,2,1,0:T(8,128)} copy(f32[8,2,8,2,8,16,8]{5,6,3,1,4,2,0:T(8,128)} %convolution_bitcast_fusion.1) | data formatting | bytes 2097152 | tf_op jit(solution)/shard_map/sxyz,slijk->lxiyjzk/transpose | solution.py:110
  84.0 11.8 %reshape.119 = f32[8,16,16,128]{3,2,1,0:T(8,128)S(1)} reshape(f32[8,2,8,2,8,16,8]{6,5,4,3,2,1,0:T(8,128)} %copy.25) | data formatting | bytes 2097152 | tf_op jit(solution)/shard_map/reshape | solution.py:113
  98.0 4.5 %collective-permute-start.1 = (f32[8,1,16,128]{3,2,1,0:T(8,128)S(1)}, f32[8,1,16,128]{3,2,1,0:T(8,128)S(1)}, u32[]{:S(2)}, u32[]{:S(2)}) collective-permute-start(f32[8,1,16,128]{3,2,1,0:T(8,128)S(1)} %get-tuple-element.42), channel_id=1, source_target_pairs={{16,0},{17,1},{18,2},{19,3},{20,4},{21,5},{22,6},{23,7},{24,8},{25... | collective-permute-start | bytes 196616 | tf_op jit(solution)/shard_map/ppermute | solution.py:26
  107.2 2.2 collective-permute-start.7
  113.1 2.4 fusion.112
  115.5 2.4 copy.28
  117.9 2.7 collective-permute-start.11
  120.6 2.4 copy.26
  123.0 3.1 collective-permute-start.9
  128.1 2.2 copy.29
  130.3 2.2 copy.27
  132.5 6.0 %multiply_reduce_fusion.1 = (f32[8]{0:T(128)}, f32[8]{0:T(128)}, f32[8,16,16,128]{3,2,1,0:T(8,128)S(1)}) fusion(f32[8,16,16,128]{3,2,1,0:T(8,128)S(1)} %reshape.119, f32[8,16,16,128]{3,2,1,0:T(8,128)S(1)} %copy-done.1, f32[16,16,128]{2,1,0:T(8,128)S(1)} %mul.300, f32[8,18,1,128]{3,2,1,0:T(1,128)} %copy-done.33, f32[8,18,16,128]{3,2,1,0:T(8,128)} %copy-done.7, ...), kind=kLoop, calls=%fused_computation.104 | loop fusion | flops 8912880 | bytes 5673280 | tf_op jit(solution)/shard_map/reduce_sum | solution.py:47
  138.5 30.7 %all-reduce.1 = (f32[8]{0:T(128)}, f32[8]{0:T(128)}) all-reduce(f32[8]{0:T(128)} %get-tuple-element.10, f32[8]{0:T(128)} %get-tuple-element.9), channel_id=1, replica_groups=mesh['span'=2,'height'=4,'depth'=4] {'height','depth'}, use_global_device_ids=true, to_apply=%region_3.4 | all-reduce | flops 16 | bytes 128 | tf_op jit(solution)/shard_map/psum | solution.py:15
  169.2 6.0 %all-reduce.3 = (f32[8]{0:T(128)}, f32[8]{0:T(128)}) all-reduce(f32[8]{0:T(128)} %get-tuple-element.13, f32[8]{0:T(128)} %get-tuple-element.14), channel_id=1, replica_groups=mesh['span'=2,'height'=4,'depth'=4] {'span'}, use_global_device_ids=true, to_apply=%region_4.5 | all-reduce | flops 16 | bytes 128 | tf_op jit(solution)/shard_map/psum | solution.py:15
  177.4 11.9 %reshape.121 = bf16[8,2,8,2,8,16,8]{6,5,4,3,2,1,0:T(8,128)(2,1)} reshape(bf16[8,16,16,128]{3,2,1,0:T(8,128)(2,1)} %fusion.87) | data formatting | bytes 1048576 | tf_op jit(solution)/shard_map/reshape | solution.py:99
  189.3 6.2 %bitcast_convert_fusion = bf16[16,8,8,8,8]{0,4,3,2,1:T(8,128)(2,1)S(1)} fusion(bf16[8,2,8,2,8,16,8]{6,5,4,3,2,1,0:T(8,128)(2,1)} %reshape.121, f32[2,2,16]{2,1,0:T(2,128)} %copy-done.41, s32[2,2,16]{2,1,0:T(2,128)} %copy-done.44), kind=kOutput, calls=%fused_computation.2 | convolution fusion | flops 8456192 | bytes 655872 | tf_op jit(solution)/shard_map/sxyz,lxiyjzk->slijk/dot_general | solution.py:102
  195.9 6.9 %all_to_all.20 = bf16[16,8,512]{2,1,0:T(8,128)(2,1)S(1)} all-to-all(bf16[16,8,512]{2,1,0:T(8,128)(2,1)S(1)} %copy.31), channel_id=1, replica_groups=mesh['span'=2,'height'=4,'depth'=4] {'span'}, dimensions={0} | all-to-all | bytes 262144 | tf_op jit(solution)/shard_map/all_to_all | solution.py:107
  202.8 5.6 %fusion.124 = f32[16,8,512]{2,1,0:T(8,128)S(1)} fusion(bf16[16,8,512]{2,1,0:T(8,128)(2,1)S(1)} %all_to_all.20, bf16[16,512,512]{2,1,0:T(8,128)(2,1)} %param.9), kind=kOutput, calls=%fused_computation.251 | convolution fusion | flops 67108864 | bytes 8781824 | tf_op jit(solution)/shard_map/sij,slj->sli/dot_general | solution.py:95
  208.4 7.7 %all_to_all.21 = f32[16,8,512]{2,1,0:T(8,128)S(1)} all-to-all(f32[16,8,512]{2,1,0:T(8,128)S(1)} %fusion.124), channel_id=1, replica_groups=mesh['span'=2,'height'=4,'depth'=4] {'span'}, dimensions={0} | all-to-all | bytes 524288 | tf_op jit(solution)/shard_map/all_to_all | solution.py:96
  218.1 10.1 %convolution_bitcast_fusion = f32[8,2,8,2,8,16,8]{5,6,3,1,4,2,0:T(8,128)} fusion(f32[16,8,8,8,8,1,1]{0,4,6,5,3,2,1:T(8,128)} %bitcast.147, f32[2,2,16]{2,1,0:T(2,128)S(1)} %copy-done.43, s32[2,2,16]{2,1,0:T(2,128)S(1)} %copy-done.45), kind=kOutput, calls=%fused_computation | convolution fusion | flops 50333696 | bytes 1311232 | tf_op jit(solution)/shard_map/sxyz,slijk->lxiyjzk/dot_general | solution.py:110
  228.1 12.3 %copy.33 = f32[8,2,8,2,8,16,8]{6,5,4,3,2,1,0:T(8,128)} copy(f32[8,2,8,2,8,16,8]{5,6,3,1,4,2,0:T(8,128)} %convolution_bitcast_fusion) | data formatting | bytes 2097152 | tf_op jit(solution)/shard_map/sxyz,slijk->lxiyjzk/transpose | solution.py:110
  240.4 11.9 %reshape.124 = f32[8,16,16,128]{3,2,1,0:T(8,128)S(1)} reshape(f32[8,2,8,2,8,16,8]{6,5,4,3,2,1,0:T(8,128)} %copy.33) | data formatting | bytes 2097152 | tf_op jit(solution)/shard_map/reshape | solution.py:113
  254.3 4.5 collective-permute-start.25
  260.2 4.5 %collective-permute-start.12 = (f32[8,1,16,128]{3,2,1,0:T(8,128)S(1)}, f32[8,1,16,128]{3,2,1,0:T(8,128)S(1)}, u32[]{:S(2)}, u32[]{:S(2)}) collective-permute-start(f32[8,1,16,128]{3,2,1,0:T(8,128)S(1)} %get-tuple-element.38), channel_id=1, source_target_pairs={{16,0},{17,1},{18,2},{19,3},{20,4},{21,5},{22,6},{23,7},{24,8},{25... | collective-permute-start | bytes 196616 | tf_op jit(solution)/shard_map/ppermute | solution.py:26
  265.4 2.2 constant_dynamic-update-slice_fusion.4
  269.6 2.4 collective-permute-start.15
  272.1 3.2 collective-permute-start.27
  278.4 2.4 fusion.111
  280.7 3.1 copy.36
  283.8 2.4 collective-permute-start.17
  286.2 3.0 copy.34
  289.2 4.1 collective-permute-start.16
  294.1 3.2 copy.37
  297.3 3.1 copy.35
  300.4 5.0 %fusion.22 = f32[8]{0:T(128)S(1)} fusion(f32[8,16,16,128]{3,2,1,0:T(8,128)S(1)} %reshape.124, f32[8,18,18,1]{3,2,1,0:T(8,128)} %copy.37, f32[8,18,1,128]{3,2,1,0:T(1,128)S(1)} %collective-permute-done.14, f32[8,18,16,128]{3,2,1,0:T(8,128)} %copy-done.8, f32[8,18,1,128]{3,2,1,0:T(1,128)} %copy-done.35, f32[8,18,18,1]{3,2,1,0:T(8,128)} %copy.35, ...), kind=kLoop, calls=%fused_computation.48 | loop fusion | flops 8126456 | bytes 3445024 | tf_op jit(solution)/shard_map/reduce_sum | solution.py:47
  305.5 30.6 %all-reduce = (f32[8]{0:T(128)S(1)}, f32[8]{0:T(128)S(1)}) all-reduce(f32[8]{0:T(128)S(1)} %copy-done.59, f32[8]{0:T(128)S(1)} %fusion.22), channel_id=1, replica_groups=mesh['span'=2,'height'=4,'depth'=4] {'height','depth'}, use_global_device_ids=true, to_apply=%region_9.10 | all-reduce | flops 16 | bytes 128 | tf_op jit(solution)/shard_map/psum | solution.py:15
  336.1 4.9 %all-reduce.2 = (f32[8]{0:T(128)S(1)}, f32[8]{0:T(128)S(1)}) all-reduce(f32[8]{0:T(128)S(1)} %get-tuple-element.11, f32[8]{0:T(128)S(1)} %get-tuple-element.12), channel_id=1, replica_groups=mesh['span'=2,'height'=4,'depth'=4] {'span'}, use_global_device_ids=true, to_apply=%region_10.11 | all-reduce | flops 16 | bytes 128 | tf_op jit(solution)/shard_map/psum | solution.py:15
  342.0 3.4 collective-permute-start.18
  347.8 3.2 collective-permute-start.29
  351.1 2.6 collective-permute-start.28
  355.7 2.4 collective-permute-start.21
  363.5 3.0 copy.38
  366.5 3.2 collective-permute-start.22
  371.3 2.6 collective-permute-start.23
  377.8 2.2 copy.41
  380.0 3.2 fusion.5
  385.2 41.3 %pmax.7 = f32[]{:T(128)} all-reduce(f32[]{:T(128)} %get-tuple-element.19), channel_id=1, replica_groups=mesh['span'=2,'height'=4,'depth'=4] {'span','height','depth'}, use_global_device_ids=true, to_apply=%region_21.22 | all-reduce | flops 1 | bytes 8 | tf_op jit(solution)/shard_map/pmax | solution.py:145
  430.6 4.2 collective-permute-done.30
  436.8 2.4 collective-permute-start.32
  439.2 2.6 collective-permute-done.32
  441.9 3.6 collective-permute-start.35
  445.5 2.3 collective-permute-start.34
  448.6 3.6 collective-permute-done.34
  (231 shorter events, 65.6 us)
Async XLA Ops:
  5.8 15.1 %collective-permute-start = (f32[2,1,16,128]{3,2,1,0:T(8,128)S(1)}, f32[2,1,16,128]{3,2,1,0:T(8,128)S(1)}, u32[]{:S(2)}, u32[]{:S(2)}) collective-permute-start(f32[2,1,16,128]{3,2,1,0:T(8,128)S(1)} %get-tuple-element.53), channel_id=1, source_target_pairs={{16,0},{17,1},{18,2},{19,3},{20,4},{21,5},{22,6},{23,7},{24,8},{25... | collective-permute-start | bytes 49160 | tf_op jit(solution)/shard_map/ppermute | solution.py:26
  8.2 12.6 %collective-permute-start.2 = (f32[2,1,16,128]{3,2,1,0:T(8,128)S(1)}, f32[2,1,16,128]{3,2,1,0:T(8,128)S(1)}, u32[]{:S(2)}, u32[]{:S(2)}) collective-permute-start(f32[2,1,16,128]{3,2,1,0:T(8,128)S(1)} %get-tuple-element.52), channel_id=1, source_target_pairs={{0,16},{1,17},{2,18},{3,19},{4,20},{5,21},{6,22},{7,23},{8,24},{9,... | collective-permute-start | bytes 49160 | tf_op jit(solution)/shard_map/ppermute | solution.py:23
  10.2 15.0 %copy-start.44 = (s32[2,2,16]{2,1,0:T(2,128)}, s32[2,2,16]{2,1,0:T(2,128)S(1)}, u32[]{:S(2)}) copy-start(s32[2,2,16]{2,1,0:T(2,128)S(1)} %multiply_add_fusion.1) | copy-start | bytes 772
  10.2 15.0 %copy-start.42 = (f32[2,2,16]{2,1,0:T(2,128)S(1)}, f32[2,2,16]{2,1,0:T(2,128)}, u32[]{:S(2)}) copy-start(f32[2,2,16]{2,1,0:T(2,128)} %copy-done.41) | copy-start | bytes 772
  20.8 36.5 %copy-start.21 = (f32[2,1,16,128]{3,2,1,0:T(8,128)}, f32[2,1,16,128]{3,2,1,0:T(8,128)S(1)}, u32[]{:S(2)}) copy-start(f32[2,1,16,128]{3,2,1,0:T(8,128)S(1)} %collective-permute-done.2) | copy-start | bytes 49156
  20.9 17.6 %collective-permute-start.4 = (f32[2,18,1,128]{3,2,1,0:T(1,128)S(1)}, f32[2,18,1,128]{3,2,1,0:T(1,128)S(1)}, u32[]{:S(2)}, u32[]{:S(2)}) collective-permute-start(f32[2,18,1,128]{3,2,1,0:T(1,128)S(1)} %get-tuple-element.51), channel_id=1, source_target_pairs={{4,0},{8,4},{12,8},{5,1},{9,5},{13,9},{6,2},{10,6},{14,10},{7,3},{... | collective-permute-start | bytes 55304 | tf_op jit(solution)/shard_map/ppermute | solution.py:26
  22.8 15.7 %collective-permute-start.6 = (f32[2,18,1,128]{3,2,1,0:T(1,128)S(1)}, f32[2,18,1,128]{3,2,1,0:T(1,128)S(1)}, u32[]{:S(2)}, u32[]{:S(2)}) collective-permute-start(f32[2,18,1,128]{3,2,1,0:T(1,128)S(1)} %get-tuple-element.50), channel_id=1, source_target_pairs={{0,4},{4,8},{8,12},{1,5},{5,9},{9,13},{2,6},{6,10},{10,14},{3,7},{... | collective-permute-start | bytes 55304 | tf_op jit(solution)/shard_map/ppermute | solution.py:23
  32.5 13.9 %all-to-all-start = ((bf16[16,8,512]{2,1,0:T(8,128)(2,1)}), bf16[16,8,512]{2,1,0:T(8,128)(2,1)S(1)}, u32[]{:S(2)}, u32[]{:S(2)}) async-start(bf16[16,8,512]{2,1,0:T(8,128)(2,1)} %copy.23), calls=%async_computation | async-start | bytes 262144 | tf_op jit(solution)/shard_map/all_to_all | solution.py:107
  38.5 14.3 %copy-start.27 = (f32[2,18,1,128]{3,2,1,0:T(1,128)}, f32[2,18,1,128]{3,2,1,0:T(1,128)S(1)}, u32[]{:S(2)}) copy-start(f32[2,18,1,128]{3,2,1,0:T(1,128)S(1)} %collective-permute-done.4) | copy-start | bytes 55300
  38.5 18.8 %copy-start.30 = (f32[2,18,1,128]{3,2,1,0:T(1,128)}, f32[2,18,1,128]{3,2,1,0:T(1,128)S(1)}, u32[]{:S(2)}) copy-start(f32[2,18,1,128]{3,2,1,0:T(1,128)S(1)} %collective-permute-done.6) | copy-start | bytes 55300
  39.6 69.7 %collective-permute-start.10 = (f32[2,18,18,1]{3,2,1,0:T(8,128)}, f32[2,18,18,1]{3,2,1,0:T(8,128)}, u32[]{:S(2)}, u32[]{:S(2)}) collective-permute-start(f32[2,18,18,1]{3,2,1,0:T(8,128)} %get-tuple-element.49), channel_id=1, source_target_pairs={{0,1},{1,2},{2,3},{4,5},{5,6},{6,7},{8,9},{9,10},{10,11},{12,13},{... | collective-permute-start | bytes 7784 | tf_op jit(solution)/shard_map/ppermute | solution.py:23
  43.1 14.2 %copy-start.4 = (f32[16,16,128]{2,1,0:T(8,128)S(1)}, f32[16,16,128]{2,1,0:T(8,128)}, u32[]{:S(2)}) copy-start(f32[16,16,128]{2,1,0:T(8,128)} %param.6) | copy-start | bytes 393220
  43.1 83.0 %collective-permute-start.8 = (f32[2,18,18,1]{3,2,1,0:T(8,128)}, f32[2,18,18,1]{3,2,1,0:T(8,128)}, u32[]{:S(2)}, u32[]{:S(2)}) collective-permute-start(f32[2,18,18,1]{3,2,1,0:T(8,128)} %get-tuple-element.48), channel_id=1, source_target_pairs={{1,0},{2,1},{3,2},{5,4},{6,5},{7,6},{9,8},{10,9},{11,10},{13,12},{... | collective-permute-start | bytes 7784 | tf_op jit(solution)/shard_map/ppermute | solution.py:26
  52.7 7.9 %all-to-all-start.1 = ((f32[16,8,512]{2,1,0:T(8,128)}), f32[16,8,512]{2,1,0:T(8,128)}, u32[]{:S(2)}, u32[]{:S(2)}) async-start(f32[16,8,512]{2,1,0:T(8,128)} %fusion.123), calls=%async_computation.1 | async-start | bytes 524288 | tf_op jit(solution)/shard_map/all_to_all | solution.py:96
  84.0 13.1 %copy-start.5 = (f32[16,16,128]{2,1,0:T(8,128)S(1)}, f32[16,16,128]{2,1,0:T(8,128)}, u32[]{:S(2)}) copy-start(f32[16,16,128]{2,1,0:T(8,128)} %param.6) | copy-start | bytes 393220
  84.0 13.2 %copy-start.22 = (f32[2,1,16,128]{3,2,1,0:T(8,128)S(1)}, f32[2,1,16,128]{3,2,1,0:T(8,128)}, u32[]{:S(2)}) copy-start(f32[2,1,16,128]{3,2,1,0:T(8,128)} %copy-done.21) | copy-start | bytes 49156
  84.0 13.2 %copy-start.28 = (f32[2,18,1,128]{3,2,1,0:T(1,128)S(1)}, f32[2,18,1,128]{3,2,1,0:T(1,128)}, u32[]{:S(2)}) copy-start(f32[2,18,1,128]{3,2,1,0:T(1,128)} %copy-done.27) | copy-start | bytes 55300
  95.8 13.5 %copy-start.31 = (f32[2,18,1,128]{3,2,1,0:T(1,128)S(1)}, f32[2,18,1,128]{3,2,1,0:T(1,128)}, u32[]{:S(2)}) copy-start(f32[2,18,1,128]{3,2,1,0:T(1,128)} %copy-done.30) | copy-start | bytes 55300
  95.8 6.7 %collective-permute-start.3 = (f32[8,1,16,128]{3,2,1,0:T(8,128)S(1)}, f32[8,1,16,128]{3,2,1,0:T(8,128)S(1)}, u32[]{:S(2)}, u32[]{:S(2)}) collective-permute-start(f32[8,1,16,128]{3,2,1,0:T(8,128)S(1)} %get-tuple-element.43), channel_id=1, source_target_pairs={{0,16},{1,17},{2,18},{3,19},{4,20},{5,21},{6,22},{7,23},{8,24},{9,... | collective-permute-start | bytes 196616 | tf_op jit(solution)/shard_map/ppermute | solution.py:23
  98.0 6.4 %collective-permute-start.1 = (f32[8,1,16,128]{3,2,1,0:T(8,128)S(1)}, f32[8,1,16,128]{3,2,1,0:T(8,128)S(1)}, u32[]{:S(2)}, u32[]{:S(2)}) collective-permute-start(f32[8,1,16,128]{3,2,1,0:T(8,128)S(1)} %get-tuple-element.42), channel_id=1, source_target_pairs={{16,0},{17,1},{18,2},{19,3},{20,4},{21,5},{22,6},{23,7},{24,8},{25... | collective-permute-start | bytes 196616 | tf_op jit(solution)/shard_map/ppermute | solution.py:26
  105.0 6.2 %collective-permute-start.5 = (f32[8,18,1,128]{3,2,1,0:T(1,128)S(1)}, f32[8,18,1,128]{3,2,1,0:T(1,128)S(1)}, u32[]{:S(2)}, u32[]{:S(2)}) collective-permute-start(f32[8,18,1,128]{3,2,1,0:T(1,128)S(1)} %get-tuple-element.35), channel_id=1, source_target_pairs={{4,0},{8,4},{12,8},{5,1},{9,5},{13,9},{6,2},{10,6},{14,10},{7,3},{... | collective-permute-start | bytes 221192 | tf_op jit(solution)/shard_map/ppermute | solution.py:26
  107.2 5.7 %collective-permute-start.7 = (f32[8,18,1,128]{3,2,1,0:T(1,128)S(1)}, f32[8,18,1,128]{3,2,1,0:T(1,128)S(1)}, u32[]{:S(2)}, u32[]{:S(2)}) collective-permute-start(f32[8,18,1,128]{3,2,1,0:T(1,128)S(1)} %get-tuple-element.34), channel_id=1, source_target_pairs={{0,4},{4,8},{8,12},{1,5},{5,9},{9,13},{2,6},{6,10},{10,14},{3,7},{... | collective-permute-start | bytes 221192 | tf_op jit(solution)/shard_map/ppermute | solution.py:23
  117.9 10.2 %collective-permute-start.11 = (f32[8,18,18,1]{2,0,3,1:T(8,128)S(1)}, f32[8,18,18,1]{2,0,3,1:T(8,128)S(1)}, u32[]{:S(2)}, u32[]{:S(2)}) collective-permute-start(f32[8,18,18,1]{2,0,3,1:T(8,128)S(1)} %copy.28), channel_id=1, source_target_pairs={{0,1},{1,2},{2,3},{4,5},{5,6},{6,7},{8,9},{9,10},{10,11},{12,13},{... | collective-permute-start | bytes 31112 | tf_op jit(solution)/shard_map/ppermute | solution.py:23
  123.0 7.3 %collective-permute-start.9 = (f32[8,18,18,1]{2,0,3,1:T(8,128)S(1)}, f32[8,18,18,1]{2,0,3,1:T(8,128)S(1)}, u32[]{:S(2)}, u32[]{:S(2)}) collective-permute-start(f32[8,18,18,1]{2,0,3,1:T(8,128)S(1)} %copy.26), channel_id=1, source_target_pairs={{1,0},{2,1},{3,2},{5,4},{6,5},{7,6},{9,8},{10,9},{11,10},{13,12},{... | collective-permute-start | bytes 31112 | tf_op jit(solution)/shard_map/ppermute | solution.py:26
  138.5 50.8 %copy-start.3 = (f32[8,16,16,128]{3,2,1,0:T(8,128)}, f32[8,16,16,128]{3,2,1,0:T(8,128)S(1)}, u32[]{:S(2)}) copy-start(f32[8,16,16,128]{3,2,1,0:T(8,128)S(1)} %get-tuple-element.23) | copy-start | bytes 3145732
  240.4 24.9 %copy-start.2 = (f32[8,16,16,128]{3,2,1,0:T(8,128)S(1)}, f32[8,16,16,128]{3,2,1,0:T(8,128)}, u32[]{:S(2)}) copy-start(f32[8,16,16,128]{3,2,1,0:T(8,128)} %param.5) | copy-start | bytes 3145732
  252.3 12.4 %collective-permute-start.13 = (f32[8,1,16,128]{3,2,1,0:T(8,128)S(1)}, f32[8,1,16,128]{3,2,1,0:T(8,128)S(1)}, u32[]{:S(2)}, u32[]{:S(2)}) collective-permute-start(f32[8,1,16,128]{3,2,1,0:T(8,128)S(1)} %get-tuple-element.39), channel_id=1, source_target_pairs={{0,16},{1,17},{2,18},{3,19},{4,20},{5,21},{6,22},{7,23},{8,24},{9,... | collective-permute-start | bytes 196616 | tf_op jit(solution)/shard_map/ppermute | solution.py:23
  254.3 17.7 %collective-permute-start.25 = (bf16[1,16,128]{2,1,0:T(8,128)(2,1)S(1)}, bf16[1,16,128]{2,1,0:T(8,128)(2,1)S(1)}, u32[]{:S(2)}, u32[]{:S(2)}) collective-permute-start(bf16[1,16,128]{2,1,0:T(8,128)(2,1)S(1)} %get-tuple-element.67), channel_id=1, source_target_pairs={{16,0},{17,1},{18,2},{19,3},{20,4},{21,5},{22,6},{23,7},{24,8},{25... | collective-permute-start | bytes 12296 | tf_op jit(solution)/shard_map/ppermute | solution.py:26
  258.9 13.2 %collective-permute-start.24 = (bf16[1,16,128]{2,1,0:T(8,128)(2,1)S(1)}, bf16[1,16,128]{2,1,0:T(8,128)(2,1)S(1)}, u32[]{:S(2)}, u32[]{:S(2)}) collective-permute-start(bf16[1,16,128]{2,1,0:T(8,128)(2,1)S(1)} %get-tuple-element.66), channel_id=1, source_target_pairs={{0,16},{1,17},{2,18},{3,19},{4,20},{5,21},{6,22},{7,23},{8,24},{9,... | collective-permute-start | bytes 12296 | tf_op jit(solution)/shard_map/ppermute | solution.py:23
  260.2 7.4 %collective-permute-start.12 = (f32[8,1,16,128]{3,2,1,0:T(8,128)S(1)}, f32[8,1,16,128]{3,2,1,0:T(8,128)S(1)}, u32[]{:S(2)}, u32[]{:S(2)}) collective-permute-start(f32[8,1,16,128]{3,2,1,0:T(8,128)S(1)} %get-tuple-element.38), channel_id=1, source_target_pairs={{16,0},{17,1},{18,2},{19,3},{20,4},{21,5},{22,6},{23,7},{24,8},{25... | collective-permute-start | bytes 196616 | tf_op jit(solution)/shard_map/ppermute | solution.py:26
  267.7 9.7 %collective-permute-start.14 = (f32[8,18,1,128]{3,2,1,0:T(1,128)S(1)}, f32[8,18,1,128]{3,2,1,0:T(1,128)S(1)}, u32[]{:S(2)}, u32[]{:S(2)}) collective-permute-start(f32[8,18,1,128]{3,2,1,0:T(1,128)S(1)} %get-tuple-element.33), channel_id=1, source_target_pairs={{4,0},{8,4},{12,8},{5,1},{9,5},{13,9},{6,2},{10,6},{14,10},{7,3},{... | collective-permute-start | bytes 221192 | tf_op jit(solution)/shard_map/ppermute | solution.py:26
  269.6 7.8 %collective-permute-start.15 = (f32[8,18,1,128]{3,2,1,0:T(1,128)S(1)}, f32[8,18,1,128]{3,2,1,0:T(1,128)S(1)}, u32[]{:S(2)}, u32[]{:S(2)}) collective-permute-start(f32[8,18,1,128]{3,2,1,0:T(1,128)S(1)} %get-tuple-element.32), channel_id=1, source_target_pairs={{0,4},{4,8},{8,12},{1,5},{5,9},{9,13},{2,6},{6,10},{10,14},{3,7},{... | collective-permute-start | bytes 221192 | tf_op jit(solution)/shard_map/ppermute | solution.py:23
  272.1 21.2 %collective-permute-start.27 = (bf16[18,1,128]{2,1,0:T(2,128)(2,1)S(1)}, bf16[18,1,128]{2,1,0:T(2,128)(2,1)S(1)}, u32[]{:S(2)}, u32[]{:S(2)}) collective-permute-start(bf16[18,1,128]{2,1,0:T(2,128)(2,1)S(1)} %get-tuple-element.63), channel_id=1, source_target_pairs={{4,0},{8,4},{12,8},{5,1},{9,5},{13,9},{6,2},{10,6},{14,10},{7,3},{... | collective-permute-start | bytes 13832 | tf_op jit(solution)/shard_map/ppermute | solution.py:26
  275.3 18.0 %collective-permute-start.26 = (bf16[18,1,128]{2,1,0:T(2,128)(2,1)S(1)}, bf16[18,1,128]{2,1,0:T(2,128)(2,1)S(1)}, u32[]{:S(2)}, u32[]{:S(2)}) collective-permute-start(bf16[18,1,128]{2,1,0:T(2,128)(2,1)S(1)} %get-tuple-element.62), channel_id=1, source_target_pairs={{0,4},{4,8},{8,12},{1,5},{5,9},{9,13},{2,6},{6,10},{10,14},{3,7},{... | collective-permute-start | bytes 13832 | tf_op jit(solution)/shard_map/ppermute | solution.py:23
  280.7 12.6 %copy-start.19 = (bf16[16,16,128]{2,1,0:T(8,128)(2,1)S(1)}, bf16[16,16,128]{2,1,0:T(8,128)(2,1)}, u32[]{:S(2)}) copy-start(bf16[16,16,128]{2,1,0:T(8,128)(2,1)} %get-tuple-element.54) | copy-start | bytes 196612
  280.7 12.6 %copy-start.47 = (bf16[1,16,128]{2,1,0:T(8,128)(2,1)S(1)}, bf16[1,16,128]{2,1,0:T(8,128)(2,1)}, u32[]{:S(2)}) copy-start(bf16[1,16,128]{2,1,0:T(8,128)(2,1)} %copy-done.46) | copy-start | bytes 12292
  280.7 12.6 %copy-start.50 = (bf16[1,16,128]{2,1,0:T(8,128)(2,1)S(1)}, bf16[1,16,128]{2,1,0:T(8,128)(2,1)}, u32[]{:S(2)}) copy-start(bf16[1,16,128]{2,1,0:T(8,128)(2,1)} %copy-done.49) | copy-start | bytes 12292
  283.8 10.3 %collective-permute-start.17 = (f32[8,18,18,1]{2,0,3,1:T(8,128)}, f32[8,18,18,1]{2,0,3,1:T(8,128)}, u32[]{:S(2)}, u32[]{:S(2)}) collective-permute-start(f32[8,18,18,1]{2,0,3,1:T(8,128)} %copy.36), channel_id=1, source_target_pairs={{0,1},{1,2},{2,3},{4,5},{5,6},{6,7},{8,9},{9,10},{10,11},{12,13},{... | collective-permute-start | bytes 31112 | tf_op jit(solution)/shard_map/ppermute | solution.py:23
  289.2 8.0 %collective-permute-start.16 = (f32[8,18,18,1]{2,0,3,1:T(8,128)}, f32[8,18,18,1]{2,0,3,1:T(8,128)}, u32[]{:S(2)}, u32[]{:S(2)}) collective-permute-start(f32[8,18,18,1]{2,0,3,1:T(8,128)} %copy.34), channel_id=1, source_target_pairs={{1,0},{2,1},{3,2},{5,4},{6,5},{7,6},{9,8},{10,9},{11,10},{13,12},{... | collective-permute-start | bytes 31112 | tf_op jit(solution)/shard_map/ppermute | solution.py:26
  300.4 40.6 %copy-start.60 = (f32[8]{0:T(128)S(1)}, f32[8]{0:T(128)}, u32[]{:S(2)}) copy-start(f32[8]{0:T(128)} %get-tuple-element.17) | copy-start | bytes 100
  300.4 40.6 %copy-start.61 = (f32[8]{0:T(128)S(1)}, f32[8]{0:T(128)}, u32[]{:S(2)}) copy-start(f32[8]{0:T(128)} %get-tuple-element.18) | copy-start | bytes 100
  341.9 38.0 %copy-start = (f32[8,16,16,128]{3,2,1,0:T(8,128)}, f32[8,16,16,128]{3,2,1,0:T(8,128)S(1)}, u32[]{:S(2)}) copy-start(f32[8,16,16,128]{3,2,1,0:T(8,128)S(1)} %multiply_add_fusion) | copy-start | bytes 3145732
  341.9 16.2 %copy-start.20 = (bf16[16,16,128]{2,1,0:T(8,128)(2,1)S(1)}, bf16[16,16,128]{2,1,0:T(8,128)(2,1)}, u32[]{:S(2)}) copy-start(bf16[16,16,128]{2,1,0:T(8,128)(2,1)} %get-tuple-element.54) | copy-start | bytes 196612
  341.9 16.2 %copy-start.48 = (bf16[1,16,128]{2,1,0:T(8,128)(2,1)S(1)}, bf16[1,16,128]{2,1,0:T(8,128)(2,1)}, u32[]{:S(2)}) copy-start(bf16[1,16,128]{2,1,0:T(8,128)(2,1)} %copy-done.46) | copy-start | bytes 12292
  341.9 16.2 %copy-start.51 = (bf16[1,16,128]{2,1,0:T(8,128)(2,1)S(1)}, bf16[1,16,128]{2,1,0:T(8,128)(2,1)}, u32[]{:S(2)}) copy-start(bf16[1,16,128]{2,1,0:T(8,128)(2,1)} %copy-done.49) | copy-start | bytes 12292
  342.0 16.2 %copy-start.53 = (bf16[18,1,128]{2,1,0:T(2,128)(2,1)S(1)}, bf16[18,1,128]{2,1,0:T(2,128)(2,1)}, u32[]{:S(2)}) copy-start(bf16[18,1,128]{2,1,0:T(2,128)(2,1)} %copy-done.52) | copy-start | bytes 13828
  342.0 16.2 %copy-start.55 = (bf16[18,1,128]{2,1,0:T(2,128)(2,1)S(1)}, bf16[18,1,128]{2,1,0:T(2,128)(2,1)}, u32[]{:S(2)}) copy-start(bf16[18,1,128]{2,1,0:T(2,128)(2,1)} %copy-done.54) | copy-start | bytes 13828
  342.0 11.7 %collective-permute-start.18 = (f32[8,1,16,128]{3,2,1,0:T(8,128)S(1)}, f32[8,1,16,128]{3,2,1,0:T(8,128)S(1)}, u32[]{:S(2)}, u32[]{:S(2)}) collective-permute-start(f32[8,1,16,128]{3,2,1,0:T(8,128)S(1)} %get-tuple-element.37), channel_id=1, source_target_pairs={{16,0},{17,1},{18,2},{19,3},{20,4},{21,5},{22,6},{23,7},{24,8},{25... | collective-permute-start | bytes 196616 | tf_op jit(solution)/shard_map/ppermute | solution.py:26
  345.4 8.2 %collective-permute-start.19 = (f32[8,1,16,128]{3,2,1,0:T(8,128)S(1)}, f32[8,1,16,128]{3,2,1,0:T(8,128)S(1)}, u32[]{:S(2)}, u32[]{:S(2)}) collective-permute-start(f32[8,1,16,128]{3,2,1,0:T(8,128)S(1)} %get-tuple-element.36), channel_id=1, source_target_pairs={{0,16},{1,17},{2,18},{3,19},{4,20},{5,21},{6,22},{7,23},{8,24},{9,... | collective-permute-start | bytes 196616 | tf_op jit(solution)/shard_map/ppermute | solution.py:23
  347.8 10.3 %collective-permute-start.29 = (bf16[18,18,1]{2,1,0:T(8,128)(2,1)S(1)}, bf16[18,18,1]{2,1,0:T(8,128)(2,1)S(1)}, u32[]{:S(2)}, u32[]{:S(2)}) collective-permute-start(bf16[18,18,1]{2,1,0:T(8,128)(2,1)S(1)} %get-tuple-element.59), channel_id=1, source_target_pairs={{1,0},{2,1},{3,2},{5,4},{6,5},{7,6},{9,8},{10,9},{11,10},{13,12},{... | collective-permute-start | bytes 1952 | tf_op jit(solution)/shard_map/ppermute | solution.py:26
  351.1 7.1 %collective-permute-start.28 = (bf16[18,18,1]{2,1,0:T(8,128)(2,1)S(1)}, bf16[18,18,1]{2,1,0:T(8,128)(2,1)S(1)}, u32[]{:S(2)}, u32[]{:S(2)}) collective-permute-start(bf16[18,18,1]{2,1,0:T(8,128)(2,1)S(1)} %get-tuple-element.58), channel_id=1, source_target_pairs={{0,1},{1,2},{2,3},{4,5},{5,6},{6,7},{8,9},{9,10},{10,11},{12,13},{... | collective-permute-start | bytes 1952 | tf_op jit(solution)/shard_map/ppermute | solution.py:23
  353.8 5.4 %collective-permute-start.20 = (f32[8,18,1,128]{3,2,1,0:T(1,128)S(1)}, f32[8,18,1,128]{3,2,1,0:T(1,128)S(1)}, u32[]{:S(2)}, u32[]{:S(2)}) collective-permute-start(f32[8,18,1,128]{3,2,1,0:T(1,128)S(1)} %get-tuple-element.31), channel_id=1, source_target_pairs={{4,0},{8,4},{12,8},{5,1},{9,5},{13,9},{6,2},{10,6},{14,10},{7,3},{... | collective-permute-start | bytes 221192 | tf_op jit(solution)/shard_map/ppermute | solution.py:26
  355.7 5.7 %collective-permute-start.21 = (f32[8,18,1,128]{3,2,1,0:T(1,128)S(1)}, f32[8,18,1,128]{3,2,1,0:T(1,128)S(1)}, u32[]{:S(2)}, u32[]{:S(2)}) collective-permute-start(f32[8,18,1,128]{3,2,1,0:T(1,128)S(1)} %get-tuple-element.30), channel_id=1, source_target_pairs={{0,4},{4,8},{8,12},{1,5},{5,9},{9,13},{2,6},{6,10},{10,14},{3,7},{... | collective-permute-start | bytes 221192 | tf_op jit(solution)/shard_map/ppermute | solution.py:23
  361.4 12.5 %copy-start.24 = (f32[8,18,1,128]{3,2,1,0:T(1,128)}, f32[8,18,1,128]{3,2,1,0:T(1,128)S(1)}, u32[]{:S(2)}) copy-start(f32[8,18,1,128]{3,2,1,0:T(1,128)S(1)} %collective-permute-done.21) | copy-start | bytes 221188
  366.5 8.4 %collective-permute-start.22 = (f32[8,18,18,1]{2,0,3,1:T(8,128)}, f32[8,18,18,1]{2,0,3,1:T(8,128)}, u32[]{:S(2)}, u32[]{:S(2)}) collective-permute-start(f32[8,18,18,1]{2,0,3,1:T(8,128)} %copy.38), channel_id=1, source_target_pairs={{1,0},{2,1},{3,2},{5,4},{6,5},{7,6},{9,8},{10,9},{11,10},{13,12},{... | collective-permute-start | bytes 31112 | tf_op jit(solution)/shard_map/ppermute | solution.py:26
  371.3 6.4 %collective-permute-start.23 = (f32[8,18,18,1]{2,0,3,1:T(8,128)}, f32[8,18,18,1]{2,0,3,1:T(8,128)S(1)}, u32[]{:S(2)}, u32[]{:S(2)}) collective-permute-start(f32[8,18,18,1]{2,0,3,1:T(8,128)} %copy.40), channel_id=1, source_target_pairs={{0,1},{1,2},{2,3},{4,5},{5,6},{6,7},{8,9},{9,10},{10,11},{12,13},{... | collective-permute-start | bytes 31112 | tf_op jit(solution)/shard_map/ppermute | solution.py:23
  383.2 44.0 %copy-start.9 = (f32[18,18,130]{2,1,0:T(8,128)S(1)}, f32[18,18,130]{2,1,0:T(8,128)}, u32[]{:S(2)}) copy-start(f32[18,18,130]{2,1,0:T(8,128)} %maximum_convert_fusion) | copy-start | bytes 505444
  385.2 68.0 %copy-start.17 = (f32[16,16,128]{2,1,0:T(8,128)}, f32[16,16,128]{2,1,0:T(8,128)S(1)}, u32[]{:S(2)}) copy-start(f32[16,16,128]{2,1,0:T(8,128)S(1)} %get-tuple-element.20) | copy-start | bytes 393220
  427.5 3.1 collective-permute-start.31
  429.3 5.5 %collective-permute-start.30 = (bf16[1,16,128]{2,1,0:T(8,128)(2,1)S(1)}, bf16[1,16,128]{2,1,0:T(8,128)(2,1)S(1)}, u32[]{:S(2)}, u32[]{:S(2)}) collective-permute-start(bf16[1,16,128]{2,1,0:T(8,128)(2,1)S(1)} %get-tuple-element.64), channel_id=1, source_target_pairs={{0,16},{1,17},{2,18},{3,19},{4,20},{5,21},{6,22},{7,23},{8,24},{9,... | collective-permute-start | bytes 12296 | tf_op jit(solution)/shard_map/ppermute | solution.py:23
  434.8 4.3 collective-permute-start.33
  436.8 5.0 %collective-permute-start.32 = (bf16[18,1,128]{2,1,0:T(2,128)(2,1)S(1)}, bf16[18,1,128]{2,1,0:T(2,128)(2,1)S(1)}, u32[]{:S(2)}, u32[]{:S(2)}) collective-permute-start(bf16[18,1,128]{2,1,0:T(2,128)(2,1)S(1)} %get-tuple-element.60), channel_id=1, source_target_pairs={{0,4},{4,8},{8,12},{1,5},{5,9},{9,13},{2,6},{6,10},{10,14},{3,7},{... | collective-permute-start | bytes 13832 | tf_op jit(solution)/shard_map/ppermute | solution.py:23
  441.9 6.6 %collective-permute-start.35 = (bf16[18,18,1]{2,1,0:T(8,128)(2,1)S(1)}, bf16[18,18,1]{2,1,0:T(8,128)(2,1)S(1)}, u32[]{:S(2)}, u32[]{:S(2)}) collective-permute-start(bf16[18,18,1]{2,1,0:T(8,128)(2,1)S(1)} %get-tuple-element.57), channel_id=1, source_target_pairs={{1,0},{2,1},{3,2},{5,4},{6,5},{7,6},{9,8},{10,9},{11,10},{13,12},{... | collective-permute-start | bytes 1952 | tf_op jit(solution)/shard_map/ppermute | solution.py:26
  445.5 6.6 %collective-permute-start.34 = (bf16[18,18,1]{2,1,0:T(8,128)(2,1)S(1)}, bf16[18,18,1]{2,1,0:T(8,128)(2,1)S(1)}, u32[]{:S(2)}, u32[]{:S(2)}) collective-permute-start(bf16[18,18,1]{2,1,0:T(8,128)(2,1)S(1)} %get-tuple-element.56), channel_id=1, source_target_pairs={{0,1},{1,2},{2,3},{4,5},{5,6},{6,7},{8,9},{9,10},{10,11},{12,13},{... | collective-permute-start | bytes 1952 | tf_op jit(solution)/shard_map/ppermute | solution.py:23
  (36 other events, 177.7 us)
